TPU v7x, 32 devices: a whole 2x2x4 slice. The times are simulated.
32 devices in a mesh: tp: 4 (over z), dp: 8 (over y, x, core).
Axes of the slice: x: 2, y: 2, z: 4, core: 2. Of those that a mesh axis runs over, the one named last changes fastest.
Arguments:
- hidden: bfloat16 [2048, 896], P('dp')
- norm_w: bfloat16 [896], replicated
- emb_table: bfloat16 [151936, 896], P('tp')
- teacher: bfloat16 [2048, 151936], P('dp', 'tp')
- loss_mask: int32 [2048], P('dp')
Outputs:
- output 1: float32 [], replicated
- output 2: bfloat16 [2048, 896], P('dp')
- output 3: float32 [151936, 896], P('tp', 'dp')
- output 4: float32 [896], replicated
All inputs are finite; a program needn't handle non-finite values.
Results may differ from a plain program's by a relative error of at most 0.001.
Values sent between devices are 32-bit elements.
A program may use at most 1 GiB of HBM per device.

v0:
```python
import jax
import jax.numpy as jnp
from jax import lax
from jax.sharding import PartitionSpec as P

SOFT_CAP = 30.0
NORM_EPS = 1e-6


def rms_norm(hid_f32, scale_f32):
    inv_rms = lax.rsqrt(jnp.mean(hid_f32 * hid_f32, axis=-1, keepdims=True) + NORM_EPS)
    return hid_f32 * inv_rms * (1.0 + scale_f32)


def solution(mesh):
    def device_fn(hid_loc, norm_w, emb_loc, teach_loc, mask_loc):
        mask_f32 = mask_loc.astype(jnp.float32)
        tok_count = lax.psum(jnp.sum(mask_f32), 'dp')
        weight = mask_f32 / tok_count
        normed_f32, norm_pull = jax.vjp(rms_norm, hid_loc.astype(jnp.float32), norm_w.astype(jnp.float32))
        normed = normed_f32.astype(jnp.bfloat16)
        raw_logit = jnp.einsum('nd,vd->nv', normed, emb_loc, preferred_element_type=jnp.float32)
        tanh_val = jnp.tanh(raw_logit / SOFT_CAP)
        capped = SOFT_CAP * tanh_val
        teach_f32 = teach_loc.astype(jnp.float32)
        maxima = lax.pmax(jnp.stack([jnp.max(capped, axis=-1), jnp.max(teach_f32, axis=-1)], axis=-1), 'tp')
        stu_exp = jnp.exp(capped - maxima[:, 0:1])
        tea_exp = jnp.exp(teach_f32 - maxima[:, 1:2])
        local_sums = jnp.stack([jnp.sum(stu_exp, axis=-1), jnp.sum(tea_exp, axis=-1), jnp.sum(tea_exp * (teach_f32 - capped), axis=-1)], axis=-1)
        totals = lax.psum(local_sums, 'tp')
        lse_stu = maxima[:, 0] + jnp.log(totals[:, 0])
        lse_tea = maxima[:, 1] + jnp.log(totals[:, 1])
        kl_tok = totals[:, 2] / totals[:, 1] - lse_tea + lse_stu
        loss_val = lax.psum(jnp.sum(weight * kl_tok), 'dp')
        prob_diff = stu_exp / totals[:, 0:1] - tea_exp / totals[:, 1:2]
        d_raw = (prob_diff * weight[:, None] * (1.0 - tanh_val * tanh_val)).astype(jnp.bfloat16)
        grad_normed = lax.psum(jnp.dot(d_raw, emb_loc, preferred_element_type=jnp.float32), 'tp')
        emb_part = jnp.einsum('nv,nd->vd', d_raw, normed, preferred_element_type=jnp.float32)
        grad_emb = lax.psum_scatter(emb_part, 'dp', scatter_dimension=1, tiled=True)
        grad_hid, grad_scale = norm_pull(grad_normed)
        grad_w = lax.psum(grad_scale, 'dp')
        return loss_val, grad_hid.astype(jnp.bfloat16), grad_emb, grad_w

    return jax.shard_map(device_fn, mesh=mesh, in_specs=(P('dp', None), P(None), P('tp', None), P('dp', 'tp'), P('dp')), out_specs=(P(), P('dp', None), P('tp', 'dp'), P(None)), check_vma=False)
```

profile of v0, /device:TPU:0, one launch (start us, length us, event | category | flops | bytes accessed | tf_op | source)
XLA Modules:
  0.0 2019.0 jit_solution(6659956091121427058)
XLA Ops:
  7.2 0.0 all-reduce.5.cloned.1.call-start
  7.2 11.2 reduce_max.26
  18.4 0.7 convert_add_fusion
  19.1 1.2 fusion.17
  20.3 0.0 copy-start.1
  20.3 42.1 %multiply_reduce_fusion = (f32[256]{0:T(256)S(1)}, f32[256,37984]{0,1:T(8,128)}) fusion(bf16[37984,896]{1,0:T(8,128)(2,1)} %param.7, bf16[256,896]{1,0:T(8,128)(2,1)} %param.5, f32[896]{0:T(1024)S(1)} %convert_add_fusion, f32[256]{0:T(256)S(1)} %fusion.22), kind=kOutput, calls=%fused_computation.15 | convolution fusion | flops 17455325184 | bytes 107427328 | tf_op jit(solution)/shard_map/nd,vd->nv/dot_general | solution.py:22
  62.4 0.0 copy-done.1
  62.4 0.0 copy-start.3
  62.4 13.5 pmax.7
  76.0 24.0 %fusion.11 = (f32[256]{0:T(256)S(1)}, f32[256]{0:T(256)S(1)}, f32[256]{0:T(256)S(1)}) fusion(f32[256,37984]{0,1:T(8,128)} %get-tuple-element.19, f32[256]{0:T(256)S(1)} %bitcast.21, f32[256]{0:T(256)S(1)} %bitcast.18, bf16[256,37984]{0,1:T(8,128)(2,1)} %param.8), kind=kLoop, calls=%fused_computation.14 | loop fusion | flops 87514368 | bytes 58348544 | tf_op jit(solution)/shard_map/reduce_sum | solution.py:29
  100.0 8.4 psum.36
  108.4 0.0 copy-done.3
  108.4 0.6 convert_reduce_fusion
  109.0 12.6 psum.35
  121.6 1.3 multiply_reduce_fusion.1
  122.9 0.0 copy-start
  122.9 32.7 %fusion.10 = bf16[256,37984]{0,1:T(8,128)(2,1)} fusion(f32[256,37984]{0,1:T(8,128)} %get-tuple-element.19, bf16[256,37984]{0,1:T(8,128)(2,1)} %param.8, f32[256]{0:T(256)S(1)} %get-tuple-element.12, f32[256]{0:T(256)S(1)} %bitcast.27, f32[256]{0:T(256)S(1)} %bitcast.25, f32[256]{0:T(256)S(1)} %bitcast.20, f32[256]{0:T(256)S(1)} %bitcast.23), kind=kLoop, calls=%fused_computation.13 | loop fusion | flops 116686848 | bytes 77796352 | tf_op jit(solution)/shard_map/convert_element_type | solution.py:36
  155.7 0.0 copy-done
  155.7 52.2 %fusion.19 = f32[37984,896]{0,1:T(8,128)} fusion(bf16[256,37984]{0,1:T(8,128)(2,1)} %fusion.10, bf16[256,896]{1,0:T(8,128)(2,1)S(1)} %copy-done, f32[896]{0:T(1024)S(1)} %convert_add_fusion, f32[256]{0:T(256)S(1)} %fusion.22), kind=kOutput, calls=%fused_computation.28 | convolution fusion | flops 17426153472 | bytes 156045824 | tf_op jit(solution)/shard_map/nv,nd->vd/dot_general | solution.py:38
  207.8 1500.1 %fusion = f32[37984,128]{0,1:T(8,128)} fusion(f32[37984,896]{0,1:T(8,128)} %fusion.19), kind=kCustom, calls=%all-reduce-scatter | all-reduce-scatter fusion | flops 38895616 | bytes 155582976
  1708.0 11.6 slice.30
  1719.6 0.0 copy-start.4
  1719.6 0.0 copy-start.2
  1719.6 7.4 collective-permute-start
  1726.9 32.2 %fusion.25 = f32[256,896]{1,0:T(8,128)} fusion(bf16[256,37984]{0,1:T(8,128)(2,1)} %fusion.10, bf16[37984,896]{1,0:T(8,128)(2,1)} %param.7), kind=kOutput, calls=%fused_computation.41 | convolution fusion | flops 17425235968 | bytes 88432640 | tf_op jit(solution)/shard_map/dot_general | solution.py:37
  1759.1 0.0 all-reduce.5.cloned.1.call-update
  1759.2 0.0 copy-done.4
  1759.2 0.6 dynamic-slice.4
  1760.4 44.5 %all-reduce.5.cloned.1.call-done = f32[256,896]{1,0:T(8,128)} async-done(((f32[256,896]{1,0:T(8,128)}), f32[256,896]{1,0:T(8,128)}) %all-reduce.5.cloned.1.call-update) | async-done | bytes 917520 | tf_op jit(solution)/shard_map/psum | solution.py:37
  1804.9 1.5 fusion.15
  1806.4 105.4 %all-reduce.2 = (f32[]{:T(128)}, f32[896]{0:T(1024)}) all-reduce(f32[]{:T(128)} %get-tuple-element.11, f32[896]{0:T(1024)S(1)} %get-tuple-element.7), channel_id=1, replica_groups=mesh['tp'=4,'dp'=8] {'dp'}, use_global_device_ids=true, to_apply=%region_11.0 | all-reduce | flops 897 | bytes 7176 | tf_op jit(solution)/shard_map/psum | solution.py:34
  1911.8 0.0 copy-done.2
  1911.8 2.2 fusion.16
  1914.0 0.0 collective-permute-done
  1914.0 86.5 %concatenate = f32[37984,240]{0,1:T(8,128)} concatenate(f32[37984,112]{0,1:T(8,128)} %collective-permute-done, f32[37984,128]{0,1:T(8,128)} %fusion), dimensions={1} | concatenate | bytes 72929280
  2000.5 11.6 constant_dynamic-slice_fusion
  (7 shorter events, 0.0 us)
Async XLA Ops:
  7.2 1797.8 %all-reduce.5.cloned.1.call-start = ((), (), s32[]{:S(2)}) async-start(), calls=%async_computation | async-start | bytes 1835008 | tf_op jit(solution)/shard_map/psum | solution.py:37
  20.3 42.2 %copy-start.1 = (f32[256]{0:T(256)}, f32[256]{0:T(256)S(1)}, u32[]{:S(2)}) copy-start(f32[256]{0:T(256)S(1)} %fusion.17) | copy-start | bytes 3076
  62.4 46.0 %copy-start.3 = (s32[256]{0:T(256)S(1)}, s32[256]{0:T(256)}, u32[]{:S(2)}) copy-start(s32[256]{0:T(256)} %param.9) | copy-start | bytes 3076
  122.9 32.7 %copy-start = (bf16[256,896]{1,0:T(8,128)(2,1)S(1)}, bf16[256,896]{1,0:T(8,128)(2,1)}, u32[]{:S(2)}) copy-start(bf16[256,896]{1,0:T(8,128)(2,1)} %param.5) | copy-start | bytes 1376260
  1719.6 39.6 %copy-start.4 = (u32[32]{0:T(128)S(1)}, u32[32]{0:T(128)}, u32[]{:S(2)}) copy-start(u32[32]{0:T(128)} %constant.23) | copy-start | bytes 388
  1719.6 192.2 %copy-start.2 = (f32[256]{0:T(256)S(1)}, f32[256]{0:T(256)}, u32[]{:S(2)}) copy-start(f32[256]{0:T(256)} %copy-done.1) | copy-start | bytes 3076
  1719.6 194.5 %collective-permute-start = (f32[37984,112]{0,1:T(8,128)}, f32[37984,112]{0,1:T(8,128)}, u32[]{:S(2)}, u32[]{:S(2)}) collective-permute-start(f32[37984,112]{0,1:T(8,128)} %slice.30), channel_id=1, source_target_pairs={{0,1},{1,2},{2,3},{3,4},{4,5},{5,6},{6,7},{8,9},{9,10},{10,11},{11... | collective-permute-start | bytes 51050504
Sparse Core Ops, SparseCore 0:
  1759.3 45.6 all-reduce.4
where the time goes:
time: 2020 us
  blocking collectives  1640 us (81%)
  matrix products  127 us (6%)
  local copies, waits for them, and re-layouts  110 us (5%)
  other arithmetic  75.4 us (4%)
  waiting for transfers between devices  44.5 us (2%)
    unnamed x1, blocking collectives  1500 us
    unnamed x14, local copies, waits for them, and re-layouts  110 us
    psum x1, blocking collectives, device_fn(): loss_val = lax.psum(jnp.sum(weight * kl_tok), 'dp')  105 us
    dot_general x1, matrix products, device_fn(): jnp.einsum('nv,nd->vd', d_raw, normed, preferred_element_type=jnp.float32)  52.2 us
    psum x1, waiting for transfers between devices, device_fn(): lax.psum(jnp.dot(d_raw, emb_loc, preferred_element_type=jnp.float32), 'tp')  44.5 us
    dot_general x1, matrix products, device_fn(): jnp.einsum('nd,vd->nv', normed, emb_loc, preferred_element_type=jnp.float32)  42.1 us
  transfers between devices with their start and end apart: 2, of which 1 were waited for; matrix products, arithmetic and copies ran while one was open for 2% of the time, Pallas kernels for 0%

commit v1 on v0

v1 whole, which is shorter than its diff:
```python
import functools

import jax
import jax.numpy as jnp
from jax import lax
from jax.experimental import pallas as pl
from jax.experimental.pallas import tpu as pltpu
from jax.sharding import PartitionSpec as P

SOFT_CAP = 30.0
NORM_EPS = 1e-6
LOG2E = 1.4426950408889634
CAP2 = SOFT_CAP * LOG2E
CHUNKS = 10
HALF = 1920
ROWS_F = 1024
ROWS_B = 960
ROWS_M = 640


def rms_norm(hid_f32, scale_f32):
    inv_rms = lax.rsqrt(jnp.mean(hid_f32 * hid_f32, axis=-1, keepdims=True) + NORM_EPS)
    return hid_f32 * inv_rms * (1.0 + scale_f32)


def sublane_sum(a):
    return jnp.sum(a, axis=0, keepdims=True)


def stats_kernel(vocab, e_ref, t_ref, g_ref, out_ref):
    i = pl.program_id(0)
    n = pl.num_programs(0)
    rows = e_ref.shape[0]

    @pl.when(i == 0)
    def _():
        out_ref[...] = jnp.zeros_like(out_ref)
        out_ref[1:2, :] = jnp.full((1, out_ref.shape[1]), -jnp.inf, jnp.float32)

    def block(ragged):
        raw = jnp.dot(e_ref[...], g_ref[...], preferred_element_type=jnp.float32)
        u = jnp.tanh(raw * (1.0 / SOFT_CAP))
        ez = jnp.exp2(u * CAP2 - CAP2)
        t = t_ref[...].astype(jnp.float32)
        if ragged:
            valid = lax.broadcasted_iota(jnp.int32, t.shape, 0) < vocab - i * rows
            t = jnp.where(valid, t, -jnp.inf)
        top_old = out_ref[1:2, :]
        top = jnp.maximum(top_old, jnp.max(t, axis=0, keepdims=True))
        et = jnp.exp2((t - top) * LOG2E)
        cross = et * (t - SOFT_CAP * u)
        if ragged:
            ez = jnp.where(valid, ez, 0.0)
            cross = jnp.where(valid, cross, 0.0)
        keep = jnp.exp2((top_old - top) * LOG2E)
        out_ref[0:1, :] += sublane_sum(ez)
        out_ref[1:2, :] = top
        out_ref[2:3, :] = out_ref[2:3, :] * keep + sublane_sum(et)
        out_ref[3:4, :] = out_ref[3:4, :] * keep + sublane_sum(cross)

    if vocab % rows:
        pl.when(i < n - 1)(lambda: block(False))
        pl.when(i == n - 1)(lambda: block(True))
    else:
        block(False)


def local_stats(emb, teach_t, g_t):
    vocab, dim = emb.shape
    tok = teach_t.shape[1]
    return pl.pallas_call(
        functools.partial(stats_kernel, vocab),
        out_shape=jax.ShapeDtypeStruct((8, tok), jnp.float32),
        grid=(pl.cdiv(vocab, ROWS_F),),
        in_specs=[
            pl.BlockSpec((ROWS_F, dim), lambda i: (i, 0)),
            pl.BlockSpec((ROWS_F, tok), lambda i: (i, 0)),
            pl.BlockSpec((dim, tok), lambda i: (0, 0)),
        ],
        out_specs=pl.BlockSpec((8, tok), lambda i: (0, 0)),
        cost_estimate=pl.CostEstimate(
            flops=2 * vocab * dim * tok, bytes_accessed=2 * vocab * (dim + tok), transcendentals=3 * vocab * tok
        ),
        name="stats",
    )(emb, teach_t, g_t)


def grad_kernel(limit, first, nb, side_ref, e_ref, t_ref, g_ref, st_ref, acc_ref, send_ref, own_ref, dg_ref):
    h, j = pl.program_id(0), pl.program_id(1)
    rows = e_ref.shape[0]

    @pl.when((h == 0) & (j == 0))
    def _():
        dg_ref[...] = acc_ref[...]

    emb = e_ref[...]
    raw = jnp.dot(emb, g_ref[...], preferred_element_type=jnp.float32)
    u = jnp.tanh(raw * (1.0 / SOFT_CAP))
    ez = jnp.exp2(u * CAP2 - CAP2)
    et = jnp.exp2((t_ref[...].astype(jnp.float32) - st_ref[1:2, :]) * LOG2E)
    dr = (ez * st_ref[0:1, :] - et * st_ref[2:3, :]) * (1.0 - u * u)
    if limit is not None:
        half = jnp.where(h == 0, 1 - side_ref[0], side_ref[0])
        left = limit - (first + half * nb + j) * rows
        dr = jnp.where(lax.broadcasted_iota(jnp.int32, dr.shape, 0) < left, dr, 0.0)
        emb = jnp.where(lax.broadcasted_iota(jnp.int32, emb.shape, 0) < left, emb, jnp.zeros_like(emb))
    dr = dr.astype(jnp.bfloat16)
    wide = dr.astype(jnp.float32)

    @pl.when(h == 0)
    def _():
        send_ref[...] = wide

    @pl.when(h == 1)
    def _():
        own_ref[...] = wide

    dg_ref[...] += lax.dot_general(dr, emb, (((0,), (0,)), ((), ())), preferred_element_type=jnp.float32)


def chunk_grad(chunk, side, emb, teach_t, g_t, stats, acc):
    vocab, dim = emb.shape
    tok = teach_t.shape[1]
    nb = HALF // ROWS_B
    first = chunk * 2 * nb
    limit = vocab if (chunk + 1) * 2 * HALF > vocab else None

    def rows_map(h, j, side_ref):
        half = jnp.where(h == 0, 1 - side_ref[0], side_ref[0])
        return first + half * nb + j, 0

    whole = lambda h, j, side_ref: (0, 0)
    half_shape = jax.ShapeDtypeStruct((HALF, tok), jnp.float32)
    return pl.pallas_call(
        functools.partial(grad_kernel, limit, first, nb),
        out_shape=(half_shape, half_shape, jax.ShapeDtypeStruct((tok, dim), jnp.float32)),
        grid_spec=pltpu.PrefetchScalarGridSpec(
            num_scalar_prefetch=1,
            grid=(2, nb),
            in_specs=[
                pl.BlockSpec((ROWS_B, dim), rows_map),
                pl.BlockSpec((ROWS_B, tok), rows_map),
                pl.BlockSpec((dim, tok), whole),
                pl.BlockSpec((8, tok), whole),
                pl.BlockSpec((tok, dim), whole),
            ],
            out_specs=(
                pl.BlockSpec((ROWS_B, tok), lambda h, j, s: (jnp.where(h == 0, j, nb - 1), 0)),
                pl.BlockSpec((ROWS_B, tok), lambda h, j, s: (jnp.where(h == 0, 0, j), 0)),
                pl.BlockSpec((tok, dim), whole),
            ),
        ),
        cost_estimate=pl.CostEstimate(
            flops=8 * HALF * dim * tok, bytes_accessed=4 * HALF * (dim + 3 * tok), transcendentals=6 * HALF * tok
        ),
        name="grad",
    )(side, emb, teach_t, g_t, stats, acc)


def table_kernel(own_ref, near_ref, core_ref, far_ref, g_ref, send_ref, keep_ref, pass_ref, held):
    part = keep_ref.shape[0]

    @pl.when(pl.program_id(0) == 0)
    def _():
        held[...] = g_ref[...].astype(jnp.bfloat16)

    dr = jnp.concatenate([r[...].astype(jnp.bfloat16) for r in (own_ref, near_ref, core_ref, far_ref)], axis=1)
    out = lax.dot_general(held[...], dr, (((1,), (1,)), ((), ())), preferred_element_type=jnp.float32)
    send_ref[...] = out[: 2 * part]
    keep_ref[...] = out[2 * part : 3 * part]
    pass_ref[...] = out[3 * part :]


def chunk_table(pieces, g_rows):
    rows, tok = pieces[0].shape
    width, depth = g_rows.shape
    part = width // 4
    shape = lambda k: jax.ShapeDtypeStruct((k * part, rows), jnp.float32)
    out_spec = lambda k: pl.BlockSpec((k * part, ROWS_M), lambda i: (0, i))
    return pl.pallas_call(
        table_kernel,
        out_shape=(shape(2), shape(1), shape(1)),
        grid=(rows // ROWS_M,),
        in_specs=[pl.BlockSpec((ROWS_M, tok), lambda i: (i, 0))] * 4 + [pl.BlockSpec((width, depth), lambda i: (0, 0))],
        out_specs=(out_spec(2), out_spec(1), out_spec(1)),
        scratch_shapes=[pltpu.VMEM((width, depth), jnp.bfloat16)],
        cost_estimate=pl.CostEstimate(
            flops=2 * width * depth * rows, bytes_accessed=4 * rows * (4 * tok + width), transcendentals=0
        ),
        name="table",
    )(*pieces, g_rows)


def solution(mesh):
    dp = mesh.shape['dp']
    bits = {'core': 1, 'x': 2, 'y': 4}

    def swap(a, axis):
        return lax.ppermute(a, 'dp', [(i, i ^ bits[axis]) for i in range(dp)])

    def device_fn(hid_loc, norm_w, emb_loc, teach_loc, mask_loc):
        vocab, dim = emb_loc.shape
        me = lax.axis_index('dp')
        place = {axis: (me // bit) % 2 for axis, bit in bits.items()}
        mask_f32 = mask_loc.astype(jnp.float32)
        tok_count = lax.psum(jnp.sum(mask_f32), 'dp')
        weight = mask_f32 / tok_count
        normed_f32, norm_pull = jax.vjp(rms_norm, hid_loc.astype(jnp.float32), norm_w.astype(jnp.float32))
        normed = lax.optimization_barrier(normed_f32.astype(jnp.bfloat16))
        g_t = normed.T
        teach_t = teach_loc.T

        g_own = normed.astype(jnp.float32)
        near = {axis: swap(g_own, axis) for axis in 'xy'}
        g_core = swap(g_own, 'core')

        def g_rows(a, b):
            g_all = jnp.concatenate([g_own, near[a], g_core, swap(near[a], 'core')], axis=0)
            cols = g_all.T.reshape(2, 2, 2, dim // 8, g_all.shape[0])
            cols = jnp.where(place['core'] == 0, cols[:, :, 0], cols[:, :, 1])
            cols = jnp.where(place['x'] == 0, cols, cols[:, ::-1])
            cols = jnp.where(place['y'] == 0, cols, cols[::-1])
            if b == 'x':
                cols = jnp.swapaxes(cols, 0, 1)
            return cols[::-1].reshape(dim // 2, g_all.shape[0])

        rows_of = {'x': g_rows('x', 'y'), 'y': g_rows('y', 'x')}

        own_stats = local_stats(emb_loc, teach_t, g_t)
        all_stats = lax.all_gather(own_stats[:4], 'tp')
        sum_stu = jnp.sum(all_stats[:, 0], axis=0)
        top = jnp.max(all_stats[:, 1], axis=0)
        scale = jnp.exp(all_stats[:, 1] - top)
        sum_tea = jnp.sum(all_stats[:, 2] * scale, axis=0)
        cross = jnp.sum(all_stats[:, 3] * scale, axis=0)
        kl_tok = cross / sum_tea - (top + jnp.log(sum_tea)) + (SOFT_CAP + jnp.log(sum_stu))
        loss_val = lax.psum(jnp.sum(weight * kl_tok), 'dp')
        stats = jnp.stack([weight / sum_stu, top, weight / sum_tea] + [jnp.zeros_like(top)] * 5)

        grad_part = jnp.zeros(hid_loc.shape, jnp.float32)
        side = {axis: place[axis].astype(jnp.int32)[None] for axis in 'xy'}
        grad_emb = jnp.zeros((dim // 8, vocab), jnp.float32)
        for chunk in range(CHUNKS):
            a, b = ('x', 'y') if chunk % 2 == 0 else ('y', 'x')
            send, own, grad_part = chunk_grad(chunk, side[a], emb_loc, teach_t, g_t, stats, grad_part)
            got = swap(send, a)
            pieces = (own, got, swap(own, 'core'), swap(got, 'core'))
            send_b, keep, give = chunk_table(pieces, rows_of[a])
            got_b = swap(send_b, b)
            mine = keep + got_b[: dim // 8]
            other = swap(give + got_b[dim // 8 :], a)
            low = jnp.where(place[a] == 0, mine, other)
            high = jnp.where(place[a] == 0, other, mine)
            start = chunk * 2 * HALF
            grad_emb = lax.dynamic_update_slice(grad_emb, low, (0, start))
            stop = min(vocab, start + 2 * HALF)
            grad_emb = lax.dynamic_update_slice(grad_emb, high[:, : stop - start - HALF], (0, start + HALF))

        grad_normed = lax.psum(grad_part, 'tp')
        grad_hid, grad_scale = norm_pull(grad_normed)
        grad_w = lax.psum(grad_scale, 'dp')
        return loss_val, grad_hid.astype(jnp.bfloat16), grad_emb.T, grad_w


    return jax.shard_map(device_fn, mesh=mesh, in_specs=(P('dp', None), P(None), P('tp', None), P('dp', 'tp'), P('dp')), out_specs=(P(), P('dp', None), P('tp', 'dp'), P(None)), check_vma=False)
```

time: 2020 us -> 719 us (0.36)
  blocking collectives: 1640 us -> 41.3 us
  Pallas kernels: 0 us -> 271 us
  waiting for transfers between devices: 44.5 us -> 273 us
  matrix products: 127 us -> 0 us
  local copies, waits for them, and re-layouts: 110 us -> 27.4 us
  starting transfers between devices: 7.39 us -> 38 us
  other arithmetic: 75.4 us -> 48.2 us
    unnamed x1 -> x0, blocking collectives: 1500 us -> none
    pallas_call x0 -> x21, Pallas kernels: none -> 271 us  [the longest x10 140 us: chunk_grad(): pl.pallas_call(functools.partial(grad_kernel, limit, first, nb), out_shap...]
    ppermute x0 -> x55, waiting for transfers between devices: none -> 247 us  [swap(): return lax.ppermute(a, 'dp', [(i, i ^ bits[axis]) for i in range(dp)])]
    dot_general x3 -> x0, matrix products: 127 us -> none  [the longest x1 52.2 us: device_fn(): jnp.einsum('nv,nd->vd', d_raw, normed, preferred_element_type=jnp.float32)]
    unnamed x14 -> x113, local copies, waits for them, and re-layouts: 110 us -> 15.7 us
    psum x1, blocking collectives: 105 us -> 14.9 us  [device_fn(): loss_val = lax.psum(jnp.sum(weight * kl_tok), 'dp')]
    ppermute x0 -> x55, starting transfers between devices: none -> 37.9 us  [swap(): return lax.ppermute(a, 'dp', [(i, i ^ bits[axis]) for i in range(dp)])]
    convert_element_type x2 -> x3, other arithmetic: 34.9 us -> 2.43 us  [the longest x1 2.18 us: device_fn(): return (loss_val, grad_hid.astype(jnp.bfloat16), grad_emb.T, grad_w)]
  transfers between devices with their start and end apart: 2 -> 56, of which waited for: 1 -> 21; matrix products, arithmetic and copies ran while one was open for 2% -> 9% of each run, Pallas kernels for 0% -> 38%
where the time goes in v1:
time: 719 us; the launch traced here: 714 us
  waiting for transfers between devices  273 us (38%)
  Pallas kernels  271 us (38%)
  other arithmetic  48.2 us (7%)
  blocking collectives  41.3 us (6%)
  starting transfers between devices  38 us (5%)
  local copies, waits for them, and re-layouts  27.4 us (4%)
  between operations  15.1 us (2%)
    ppermute x55, waiting for transfers between devices, swap(): return lax.ppermute(a, 'dp', [(i, i ^ bits[axis]) for i in range(dp)])  247 us
    pallas_call x10, Pallas kernels, chunk_grad(): pl.pallas_call(functools.partial(grad_kernel, limit, first, nb), out_shap...  140 us
    pallas_call x10, Pallas kernels, chunk_table(): pl.pallas_call(table_kernel, out_shape=(shape(2), shape(1), shape(1)), gr...  79.3 us
    pallas_call x1, Pallas kernels, local_stats(): pl.pallas_call(functools.partial(stats_kernel, vocab), out_shape=jax.Shap...  52.1 us
    ppermute x55, starting transfers between devices, swap(): return lax.ppermute(a, 'dp', [(i, i ^ bits[axis]) for i in range(dp)])  37.9 us
    psum x1, waiting for transfers between devices, device_fn(): grad_normed = lax.psum(grad_part, 'tp')  26.1 us
    unnamed x113, local copies, waits for them, and re-layouts  15.7 us
    psum x1, blocking collectives, device_fn(): loss_val = lax.psum(jnp.sum(weight * kl_tok), 'dp')  14.9 us
  transfers between devices with their start and end apart: 56, of which 21 were waited for; matrix products, arithmetic and copies ran while one was open for 9% of the time, Pallas kernels for 38%

profile of v1, /device:TPU:0, one launch (start us, length us, event | category | flops | bytes accessed | tf_op | source)
XLA Modules:
  0.0 714.5 jit_solution(15188421640756495467)
XLA Ops:
  10.8 3.1 collective-permute-start.11
  15.9 52.1 %stats.1 = f32[8,256]{1,0:T(8,128)} custom-call(bf16[37984,896]{1,0:T(8,128)(2,1)} %e_ref.21, bf16[37984,256]{1,0:T(8,128)(2,1)} %bitcast.44, bf16[896,256]{1,0:T(8,128)(2,1)} %bitcast.55), custom_call_target="tpu_custom_call" | custom-call | flops 17425235968 | bytes 87515136 | tf_op jit(solution)/shard_map/stats/pallas_call | solution.py:71
  68.7 13.4 %all-gather.1 = f32[4,4,256]{2,1,0:T(4,128)S(1)} all-gather(f32[1,4,256]{2,1,0:T(4,128)S(1)} %slice_bitcast_fusion), channel_id=2, replica_groups=mesh['tp'=4,'dp'=8] {'tp'}, dimensions={0}, use_global_device_ids=true | all-gather | bytes 20480 | tf_op jit(solution)/shard_map/all_gather | solution.py:230
  82.2 13.0 %psum.28 = f32[]{:T(128)} all-reduce(f32[]{:T(128)} %convert_reduce_fusion), channel_id=1, replica_groups=mesh['tp'=4,'dp'=8] {'dp'}, use_global_device_ids=true, to_apply=%region_1.2 | all-reduce | flops 1 | bytes 8 | tf_op jit(solution)/shard_map/psum | solution.py:206
  98.1 13.8 %grad.10 = (f32[1920,256]{1,0:T(8,128)}, f32[1920,256]{1,0:T(8,128)}, f32[256,896]{1,0:T(8,128)}) custom-call(s32[1]{0:T(128)} %bitcast.9.side_ref, bf16[37984,896]{1,0:T(8,128)(2,1)} %e_ref.21, bf16[37984,256]{1,0:T(8,128)(2,1)} %bitcast.45, bf16[896,256]{1,0:T(8,128)(2,1)} %bitcast.56, f32[8,256]{1,0:T(8,128)} %stack.16.st_ref, ...), custom_call_target="tpu_custom_call" | custom-call | flops 3523215360 | bytes 12779520 | tf_op jit(solution)/shard_map/grad/pallas_call | solution.py:134
  112.6 13.7 %grad.11 = (f32[1920,256]{1,0:T(8,128)}, f32[1920,256]{1,0:T(8,128)}, f32[256,896]{1,0:T(8,128)}) custom-call(s32[1]{0:T(128)} %bitcast.5.side_ref, bf16[37984,896]{1,0:T(8,128)(2,1)} %e_ref.21, bf16[37984,256]{1,0:T(8,128)(2,1)} %bitcast.46, bf16[896,256]{1,0:T(8,128)(2,1)} %bitcast.57, f32[8,256]{1,0:T(8,128)} %stack.16.st_ref, ...), custom_call_target="tpu_custom_call" | custom-call | flops 3523215360 | bytes 12779520 | tf_op jit(solution)/shard_map/grad/pallas_call | solution.py:134
  127.1 13.8 %grad.12 = (f32[1920,256]{1,0:T(8,128)}, f32[1920,256]{1,0:T(8,128)}, f32[256,896]{1,0:T(8,128)}) custom-call(s32[1]{0:T(128)} %bitcast.9.side_ref, bf16[37984,896]{1,0:T(8,128)(2,1)} %e_ref.21, bf16[37984,256]{1,0:T(8,128)(2,1)} %bitcast.47, bf16[896,256]{1,0:T(8,128)(2,1)} %bitcast.58, f32[8,256]{1,0:T(8,128)} %stack.16.st_ref, ...), custom_call_target="tpu_custom_call" | custom-call | flops 3523215360 | bytes 12779520 | tf_op jit(solution)/shard_map/grad/pallas_call | solution.py:134
  140.9 2.0 collective-permute-start.15
  142.9 14.9 %collective-permute-done.near_ref = f32[1920,256]{1,0:T(8,128)S(1)} collective-permute-done((f32[1920,256]{1,0:T(8,128)}, f32[1920,256]{1,0:T(8,128)S(1)}, u32[]{:S(2)}, u32[]{:S(2)}) %collective-permute-start) | collective-permute-done | bytes 1966112 | tf_op jit(solution)/shard_map/ppermute | solution.py:199
  157.9 14.5 %grad.13 = (f32[1920,256]{1,0:T(8,128)}, f32[1920,256]{1,0:T(8,128)}, f32[256,896]{1,0:T(8,128)}) custom-call(s32[1]{0:T(128)} %bitcast.5.side_ref, bf16[37984,896]{1,0:T(8,128)(2,1)} %e_ref.21, bf16[37984,256]{1,0:T(8,128)(2,1)} %bitcast.48, bf16[896,256]{1,0:T(8,128)(2,1)} %bitcast.59, f32[8,256]{1,0:T(8,128)} %stack.16.st_ref, ...), custom_call_target="tpu_custom_call" | custom-call | flops 3523215360 | bytes 12779520 | tf_op jit(solution)/shard_map/grad/pallas_call | solution.py:134
  172.9 13.9 %grad.14 = (f32[1920,256]{1,0:T(8,128)}, f32[1920,256]{1,0:T(8,128)}, f32[256,896]{1,0:T(8,128)}) custom-call(s32[1]{0:T(128)} %bitcast.9.side_ref, bf16[37984,896]{1,0:T(8,128)(2,1)} %e_ref.21, bf16[37984,256]{1,0:T(8,128)(2,1)} %bitcast.49, bf16[896,256]{1,0:T(8,128)(2,1)} %bitcast.60, f32[8,256]{1,0:T(8,128)} %stack.16.st_ref, ...), custom_call_target="tpu_custom_call" | custom-call | flops 3523215360 | bytes 12779520 | tf_op jit(solution)/shard_map/grad/pallas_call | solution.py:134
  187.8 12.3 %collective-permute-done.15.near_ref = f32[1920,256]{1,0:T(8,128)} collective-permute-done((f32[1920,256]{1,0:T(8,128)}, f32[1920,256]{1,0:T(8,128)}, u32[]{:S(2)}, u32[]{:S(2)}) %collective-permute-start.15) | collective-permute-done | bytes 1966112 | tf_op jit(solution)/shard_map/ppermute | solution.py:199
  200.1 14.0 %grad.15 = (f32[1920,256]{1,0:T(8,128)}, f32[1920,256]{1,0:T(8,128)}, f32[256,896]{1,0:T(8,128)}) custom-call(s32[1]{0:T(128)} %bitcast.5.side_ref, bf16[37984,896]{1,0:T(8,128)(2,1)} %e_ref.21, bf16[37984,256]{1,0:T(8,128)(2,1)} %bitcast.50, bf16[896,256]{1,0:T(8,128)(2,1)} %bitcast.61, f32[8,256]{1,0:T(8,128)} %stack.16.st_ref, ...), custom_call_target="tpu_custom_call" | custom-call | flops 3523215360 | bytes 12779520 | tf_op jit(solution)/shard_map/grad/pallas_call | solution.py:134
  214.7 2.4 collective-permute-done.20.near_ref
  217.1 14.5 %grad.16 = (f32[1920,256]{1,0:T(8,128)}, f32[1920,256]{1,0:T(8,128)}, f32[256,896]{1,0:T(8,128)}) custom-call(s32[1]{0:T(128)} %bitcast.9.side_ref, bf16[37984,896]{1,0:T(8,128)(2,1)} %e_ref.21, bf16[37984,256]{1,0:T(8,128)(2,1)} %bitcast.51, bf16[896,256]{1,0:T(8,128)(2,1)} %bitcast.62, f32[8,256]{1,0:T(8,128)} %stack.16.st_ref, ...), custom_call_target="tpu_custom_call" | custom-call | flops 3523215360 | bytes 12779520 | tf_op jit(solution)/shard_map/grad/pallas_call | solution.py:134
  231.8 10.4 %collective-permute-done.25.near_ref = f32[1920,256]{1,0:T(8,128)} collective-permute-done((f32[1920,256]{1,0:T(8,128)}, f32[1920,256]{1,0:T(8,128)}, u32[]{:S(2)}, u32[]{:S(2)}) %collective-permute-start.25) | collective-permute-done | bytes 1966112 | tf_op jit(solution)/shard_map/ppermute | solution.py:199
  242.2 13.8 %grad.17 = (f32[1920,256]{1,0:T(8,128)}, f32[1920,256]{1,0:T(8,128)}, f32[256,896]{1,0:T(8,128)}) custom-call(s32[1]{0:T(128)} %bitcast.5.side_ref, bf16[37984,896]{1,0:T(8,128)(2,1)} %e_ref.21, bf16[37984,256]{1,0:T(8,128)(2,1)} %bitcast.52, bf16[896,256]{1,0:T(8,128)(2,1)} %bitcast.63, f32[8,256]{1,0:T(8,128)} %stack.16.st_ref, ...), custom_call_target="tpu_custom_call" | custom-call | flops 3523215360 | bytes 12779520 | tf_op jit(solution)/shard_map/grad/pallas_call | solution.py:134
  256.6 3.3 collective-permute-done.30.near_ref
  259.9 13.8 %grad.18 = (f32[1920,256]{1,0:T(8,128)}, f32[1920,256]{1,0:T(8,128)}, f32[256,896]{1,0:T(8,128)}) custom-call(s32[1]{0:T(128)} %bitcast.9.side_ref, bf16[37984,896]{1,0:T(8,128)(2,1)} %e_ref.21, bf16[37984,256]{1,0:T(8,128)(2,1)} %bitcast.53, bf16[896,256]{1,0:T(8,128)(2,1)} %bitcast.64, f32[8,256]{1,0:T(8,128)} %stack.16.st_ref, ...), custom_call_target="tpu_custom_call" | custom-call | flops 3523215360 | bytes 12779520 | tf_op jit(solution)/shard_map/grad/pallas_call | solution.py:134
  273.8 10.5 %collective-permute-done.35.near_ref = f32[1920,256]{1,0:T(8,128)} collective-permute-done((f32[1920,256]{1,0:T(8,128)}, f32[1920,256]{1,0:T(8,128)}, u32[]{:S(2)}, u32[]{:S(2)}) %collective-permute-start.35) | collective-permute-done | bytes 1966112 | tf_op jit(solution)/shard_map/ppermute | solution.py:199
  284.4 14.1 %grad.19 = (f32[1920,256]{1,0:T(8,128)}, f32[1920,256]{1,0:T(8,128)}, f32[256,896]{1,0:T(8,128)}) custom-call(s32[1]{0:T(128)} %bitcast.5.side_ref, bf16[37984,896]{1,0:T(8,128)(2,1)} %e_ref.21, bf16[37984,256]{1,0:T(8,128)(2,1)} %bitcast.54, bf16[896,256]{1,0:T(8,128)(2,1)} %bitcast.65, f32[8,256]{1,0:T(8,128)} %stack.16.st_ref, ...), custom_call_target="tpu_custom_call" | custom-call | flops 3523215360 | bytes 12779520 | tf_op jit(solution)/shard_map/grad/pallas_call | solution.py:134
  299.1 2.8 collective-permute-done.40.near_ref
  301.8 2.4 copy.22
  304.9 20.5 %collective-permute-done.45.near_ref = f32[1920,256]{1,0:T(8,128)} collective-permute-done((f32[1920,256]{1,0:T(8,128)}, f32[1920,256]{1,0:T(8,128)}, u32[]{:S(2)}, u32[]{:S(2)}) %collective-permute-start.45) | collective-permute-done | bytes 1966112 | tf_op jit(solution)/shard_map/ppermute | solution.py:199
  325.4 26.1 %all-reduce.4.cloned.1.call-done = f32[256,896]{0,1:T(8,128)} async-done(((f32[256,896]{0,1:T(8,128)}), f32[256,896]{0,1:T(8,128)}) %all-reduce.4.cloned.1.call-update) | async-done | bytes 917520 | tf_op jit(solution)/shard_map/psum | solution.py:259
  353.8 2.2 fusion.9
  356.0 14.9 %all-reduce.1 = (f32[]{:T(128)}, f32[896]{0:T(1024)}) all-reduce(f32[]{:T(128)} %get-tuple-element.154, f32[896]{0:T(1024)S(1)} %get-tuple-element.132), channel_id=1, replica_groups=mesh['tp'=4,'dp'=8] {'dp'}, use_global_device_ids=true, to_apply=%region_8.9 | all-reduce | flops 897 | bytes 7176 | tf_op jit(solution)/shard_map/psum | solution.py:237
  370.9 2.0 copy.28
  372.9 2.8 fusion.1
  377.3 2.2 fusion.3
  387.1 7.9 %table.10 = (f32[224,1920]{1,0:T(8,128)}, f32[112,1920]{1,0:T(8,128)}, f32[112,1920]{1,0:T(8,128)}) custom-call(f32[1920,256]{1,0:T(8,128)} %get-tuple-element.74.own_ref, f32[1920,256]{1,0:T(8,128)} %copy-done.25, f32[1920,256]{1,0:T(8,128)} %collective-permute-done.1.core_ref, f32[1920,256]{1,0:T(8,128)} %collective-permute-done.2.far_ref, ...), custom_call_target="tpu_custom_call" | custom-call | flops 1761607680 | bytes 11304960 | tf_op jit(solution)/shard_map/table/pallas_call | solution.py:180
  395.6 2.5 fusion.2
  399.5 7.9 %table.11 = (f32[224,1920]{1,0:T(8,128)}, f32[112,1920]{1,0:T(8,128)}, f32[112,1920]{1,0:T(8,128)}) custom-call(f32[1920,256]{1,0:T(8,128)} %get-tuple-element.79.own_ref, f32[1920,256]{1,0:T(8,128)} %collective-permute-done.8.near_ref, f32[1920,256]{1,0:T(8,128)} %collective-permute-done.9.core_ref, f32[1920,256]{1,0:T(8,128)} %collective-permute-done.10.far_ref, ...), custom_call_target="tpu_custom_call" | custom-call | flops 1761607680 | bytes 11304960 | tf_op jit(solution)/shard_map/table/pallas_call | solution.py:180
  407.5 7.9 %table.12 = (f32[224,1920]{1,0:T(8,128)}, f32[112,1920]{1,0:T(8,128)}, f32[112,1920]{1,0:T(8,128)}) custom-call(f32[1920,256]{1,0:T(8,128)} %get-tuple-element.84.own_ref, f32[1920,256]{1,0:T(8,128)} %collective-permute-done.15.near_ref, f32[1920,256]{1,0:T(8,128)} %collective-permute-done.16.core_ref, f32[1920,256]{1,0:T(8,128)} %collective-permute-done.17.far_ref, ...), custom_call_target="tpu_custom_call" | custom-call | flops 1761607680 | bytes 11304960 | tf_op jit(solution)/shard_map/table/pallas_call | solution.py:180
  415.4 7.9 %table.13 = (f32[224,1920]{1,0:T(8,128)}, f32[112,1920]{1,0:T(8,128)}, f32[112,1920]{1,0:T(8,128)}) custom-call(f32[1920,256]{1,0:T(8,128)} %get-tuple-element.89.own_ref, f32[1920,256]{1,0:T(8,128)} %copy-done.27, f32[1920,256]{1,0:T(8,128)} %collective-permute-done.21.core_ref, f32[1920,256]{1,0:T(8,128)} %collective-permute-done.22.far_ref, ...), custom_call_target="tpu_custom_call" | custom-call | flops 1761607680 | bytes 11304960 | tf_op jit(solution)/shard_map/table/pallas_call | solution.py:180
  423.3 7.9 %table.14 = (f32[224,1920]{1,0:T(8,128)}, f32[112,1920]{1,0:T(8,128)}, f32[112,1920]{1,0:T(8,128)}) custom-call(f32[1920,256]{1,0:T(8,128)} %get-tuple-element.94.own_ref, f32[1920,256]{1,0:T(8,128)} %collective-permute-done.25.near_ref, f32[1920,256]{1,0:T(8,128)} %collective-permute-done.26.core_ref, f32[1920,256]{1,0:T(8,128)} %collective-permute-done.27.far_ref, ...), custom_call_target="tpu_custom_call" | custom-call | flops 1761607680 | bytes 11304960 | tf_op jit(solution)/shard_map/table/pallas_call | solution.py:180
  432.8 7.9 %table.15 = (f32[224,1920]{1,0:T(8,128)}, f32[112,1920]{1,0:T(8,128)}, f32[112,1920]{1,0:T(8,128)}) custom-call(f32[1920,256]{1,0:T(8,128)} %get-tuple-element.99.own_ref, f32[1920,256]{1,0:T(8,128)} %collective-permute-done.30.near_ref, f32[1920,256]{1,0:T(8,128)} %collective-permute-done.31.core_ref, f32[1920,256]{1,0:T(8,128)} %collective-permute-done.32.far_ref, ...), custom_call_target="tpu_custom_call" | custom-call | flops 1761607680 | bytes 11304960 | tf_op jit(solution)/shard_map/table/pallas_call | solution.py:180
  440.6 8.0 %table.16 = (f32[224,1920]{1,0:T(8,128)}, f32[112,1920]{1,0:T(8,128)}, f32[112,1920]{1,0:T(8,128)}) custom-call(f32[1920,256]{1,0:T(8,128)} %get-tuple-element.104.own_ref, f32[1920,256]{1,0:T(8,128)} %collective-permute-done.35.near_ref, f32[1920,256]{1,0:T(8,128)} %collective-permute-done.36.core_ref, f32[1920,256]{1,0:T(8,128)} %collective-permute-done.37.far_ref, ...), custom_call_target="tpu_custom_call" | custom-call | flops 1761607680 | bytes 11304960 | tf_op jit(solution)/shard_map/table/pallas_call | solution.py:180
  448.6 7.9 %table.17 = (f32[224,1920]{1,0:T(8,128)}, f32[112,1920]{1,0:T(8,128)}, f32[112,1920]{1,0:T(8,128)}) custom-call(f32[1920,256]{1,0:T(8,128)} %get-tuple-element.109.own_ref, f32[1920,256]{1,0:T(8,128)} %collective-permute-done.40.near_ref, f32[1920,256]{1,0:T(8,128)} %collective-permute-done.41.core_ref, f32[1920,256]{1,0:T(8,128)} %collective-permute-done.42.far_ref, ...), custom_call_target="tpu_custom_call" | custom-call | flops 1761607680 | bytes 11304960 | tf_op jit(solution)/shard_map/table/pallas_call | solution.py:180
  456.5 2.1 collective-permute-start.23
  458.6 7.9 %table.18 = (f32[224,1920]{1,0:T(8,128)}, f32[112,1920]{1,0:T(8,128)}, f32[112,1920]{1,0:T(8,128)}) custom-call(f32[1920,256]{1,0:T(8,128)} %get-tuple-element.114.own_ref, f32[1920,256]{1,0:T(8,128)} %collective-permute-done.45.near_ref, f32[1920,256]{1,0:T(8,128)} %collective-permute-done.46.core_ref, f32[1920,256]{1,0:T(8,128)} %collective-permute-done.47.far_ref, ...), custom_call_target="tpu_custom_call" | custom-call | flops 1761607680 | bytes 11304960 | tf_op jit(solution)/shard_map/table/pallas_call | solution.py:180
  467.1 8.2 %table.19 = (f32[224,1920]{1,0:T(8,128)}, f32[112,1920]{1,0:T(8,128)}, f32[112,1920]{1,0:T(8,128)}) custom-call(f32[1920,256]{1,0:T(8,128)} %get-tuple-element.119.own_ref, f32[1920,256]{1,0:T(8,128)} %collective-permute-done.50.near_ref, f32[1920,256]{1,0:T(8,128)} %collective-permute-done.51.core_ref, f32[1920,256]{1,0:T(8,128)} %collective-permute-done.52.far_ref, ...), custom_call_target="tpu_custom_call" | custom-call | flops 1761607680 | bytes 11304960 | tf_op jit(solution)/shard_map/table/pallas_call | solution.py:180
  479.5 1.9 collective-permute-start.43
  481.4 2.3 slice_add_fusion.14
  483.7 13.6 %collective-permute-done.23 = f32[224,1920]{1,0:T(8,128)} collective-permute-done((f32[224,1920]{1,0:T(8,128)}, f32[224,1920]{1,0:T(8,128)}, u32[]{:S(2)}, u32[]{:S(2)}) %collective-permute-start.23) | collective-permute-done | bytes 1720352 | tf_op jit(solution)/shard_map/ppermute | solution.py:199
  497.9 2.3 slice_add_fusion.12
  500.2 9.3 %collective-permute-done.28 = f32[224,1920]{1,0:T(8,128)} collective-permute-done((f32[224,1920]{1,0:T(8,128)}, f32[224,1920]{1,0:T(8,128)}, u32[]{:S(2)}, u32[]{:S(2)}) %collective-permute-start.28) | collective-permute-done | bytes 1720352 | tf_op jit(solution)/shard_map/ppermute | solution.py:199
  510.9 2.2 slice_add_fusion.10
  513.1 21.0 %collective-permute-done.33 = f32[224,1920]{1,0:T(8,128)S(1)} collective-permute-done((f32[224,1920]{1,0:T(8,128)}, f32[224,1920]{1,0:T(8,128)S(1)}, u32[]{:S(2)}, u32[]{:S(2)}) %collective-permute-start.33) | collective-permute-done | bytes 1720352 | tf_op jit(solution)/shard_map/ppermute | solution.py:199
  534.1 2.0 collective-permute-start.7
  537.2 9.1 %collective-permute-done.38 = f32[224,1920]{1,0:T(8,128)S(1)} collective-permute-done((f32[224,1920]{1,0:T(8,128)S(1)}, f32[224,1920]{1,0:T(8,128)S(1)}, u32[]{:S(2)}, u32[]{:S(2)}) %collective-permute-start.38) | collective-permute-done | bytes 1720352 | tf_op jit(solution)/shard_map/ppermute | solution.py:199
  548.1 22.8 %collective-permute-done.43 = f32[224,1920]{1,0:T(8,128)S(1)} collective-permute-done((f32[224,1920]{1,0:T(8,128)S(1)}, f32[224,1920]{1,0:T(8,128)S(1)}, u32[]{:S(2)}, u32[]{:S(2)}) %collective-permute-start.43) | collective-permute-done | bytes 1720352 | tf_op jit(solution)/shard_map/ppermute | solution.py:199
  571.0 2.0 collective-permute-start.19
  574.0 9.1 %collective-permute-done.48 = f32[224,1920]{1,0:T(8,128)S(1)} collective-permute-done((f32[224,1920]{1,0:T(8,128)S(1)}, f32[224,1920]{1,0:T(8,128)S(1)}, u32[]{:S(2)}, u32[]{:S(2)}) %collective-permute-start.48) | collective-permute-done | bytes 1720352 | tf_op jit(solution)/shard_map/ppermute | solution.py:199
  585.1 22.7 %collective-permute-done.53 = f32[224,1920]{1,0:T(8,128)S(1)} collective-permute-done((f32[224,1920]{1,0:T(8,128)S(1)}, f32[224,1920]{1,0:T(8,128)S(1)}, u32[]{:S(2)}, u32[]{:S(2)}) %collective-permute-start.53) | collective-permute-done | bytes 1720352 | tf_op jit(solution)/shard_map/ppermute | solution.py:199
  607.8 2.0 collective-permute-start.29
  611.0 15.3 %collective-permute-done.7 = f32[112,1920]{1,0:T(8,128)S(1)} collective-permute-done((f32[112,1920]{1,0:T(8,128)S(1)}, f32[112,1920]{1,0:T(8,128)S(1)}, u32[]{:S(2)}, u32[]{:S(2)}) %collective-permute-start.7) | collective-permute-done | bytes 860192 | tf_op jit(solution)/shard_map/ppermute | solution.py:199
  628.3 2.3 dynamic_update_slice.60
  635.7 9.1 %collective-permute-done.19 = f32[112,1920]{1,0:T(8,128)} collective-permute-done((f32[112,1920]{1,0:T(8,128)}, f32[112,1920]{1,0:T(8,128)}, u32[]{:S(2)}, u32[]{:S(2)}) %collective-permute-start.19) | collective-permute-done | bytes 860192 | tf_op jit(solution)/shard_map/ppermute | solution.py:199
  648.4 2.1 collective-permute-start.49
  653.5 9.7 %collective-permute-done.29 = f32[112,1920]{1,0:T(8,128)} collective-permute-done((f32[112,1920]{1,0:T(8,128)}, f32[112,1920]{1,0:T(8,128)}, u32[]{:S(2)}, u32[]{:S(2)}) %collective-permute-start.29) | collective-permute-done | bytes 860192 | tf_op jit(solution)/shard_map/ppermute | solution.py:199
  668.9 12.7 %collective-permute-done.39 = f32[112,1920]{1,0:T(8,128)S(1)} collective-permute-done((f32[112,1920]{1,0:T(8,128)S(1)}, f32[112,1920]{1,0:T(8,128)S(1)}, u32[]{:S(2)}, u32[]{:S(2)}) %collective-permute-start.39) | collective-permute-done | bytes 860192 | tf_op jit(solution)/shard_map/ppermute | solution.py:199
  683.7 15.3 %collective-permute-done.49 = f32[112,1920]{1,0:T(8,128)S(1)} collective-permute-done((f32[112,1920]{1,0:T(8,128)S(1)}, f32[112,1920]{1,0:T(8,128)S(1)}, u32[]{:S(2)}, u32[]{:S(2)}) %collective-permute-start.49) | collective-permute-done | bytes 860192 | tf_op jit(solution)/shard_map/ppermute | solution.py:199
  701.1 6.2 copy-done.1
  (245 shorter events, 67.2 us)
Async XLA Ops:
  7.2 344.3 %all-reduce.4.cloned.1.call-start = ((), (), s32[]{:S(2)}) async-start(), calls=%async_computation | async-start | bytes 1835008 | tf_op jit(solution)/shard_map/psum | solution.py:259
  9.1 58.9 %copy-start.2 = (bf16[256,896]{0,1:T(8,128)(2,1)}, bf16[256,896]{0,1:T(8,128)(2,1)S(1)}, u32[]{:S(2)}) copy-start(bf16[256,896]{0,1:T(8,128)(2,1)S(1)} %copy.19) | copy-start | bytes 1376260
  10.7 57.3 %copy-start.13 = (f32[256,896]{0,1:T(8,128)}, f32[256,896]{0,1:T(8,128)S(1)}, u32[]{:S(2)}) copy-start(f32[256,896]{0,1:T(8,128)S(1)} %convert_element_type.23) | copy-start | bytes 2752516
  10.8 101.2 %collective-permute-start.11 = (f32[256,896]{0,1:T(8,128)S(1)}, f32[256,896]{0,1:T(8,128)}, u32[]{:S(2)}, u32[]{:S(2)}) collective-permute-start(f32[256,896]{0,1:T(8,128)S(1)} %convert_element_type.23), channel_id=1, source_target_pairs={{0,4},{1,5},{2,6},{3,7},{4,0},{5,1},{6,2},{7,3},{8,12},{9,13},{10,... | collective-permute-start | bytes 2752520 | tf_op jit(solution)/shard_map/ppermute | solution.py:199
  13.8 112.6 %collective-permute-start.4 = (f32[256,896]{0,1:T(8,128)S(1)}, f32[256,896]{0,1:T(8,128)}, u32[]{:S(2)}, u32[]{:S(2)}) collective-permute-start(f32[256,896]{0,1:T(8,128)S(1)} %convert_element_type.23), channel_id=1, source_target_pairs={{0,1},{1,0},{2,3},{3,2},{4,5},{5,4},{6,7},{7,6},{8,9},{9,8},{10,11... | collective-permute-start | bytes 2752520 | tf_op jit(solution)/shard_map/ppermute | solution.py:199
  13.8 98.7 %collective-permute-start.3 = (f32[256,896]{0,1:T(8,128)S(1)}, f32[256,896]{0,1:T(8,128)}, u32[]{:S(2)}, u32[]{:S(2)}) collective-permute-start(f32[256,896]{0,1:T(8,128)S(1)} %convert_element_type.23), channel_id=1, source_target_pairs={{0,2},{1,3},{2,0},{3,1},{4,6},{5,7},{6,4},{7,5},{8,10},{9,11},{10,... | collective-permute-start | bytes 2752520 | tf_op jit(solution)/shard_map/ppermute | solution.py:199
  111.9 46.0 %collective-permute-start = (f32[1920,256]{1,0:T(8,128)}, f32[1920,256]{1,0:T(8,128)S(1)}, u32[]{:S(2)}, u32[]{:S(2)}) collective-permute-start(f32[1920,256]{1,0:T(8,128)} %get-tuple-element.75), channel_id=1, source_target_pairs={{0,2},{1,3},{2,0},{3,1},{4,6},{5,7},{6,4},{7,5},{8,10},{9,11},{10,... | collective-permute-start | bytes 5898248 | tf_op jit(solution)/shard_map/ppermute | solution.py:199
  112.0 15.0 %collective-permute-start.12 = (f32[256,896]{0,1:T(8,128)}, f32[256,896]{0,1:T(8,128)}, u32[]{:S(2)}, u32[]{:S(2)}) collective-permute-start(f32[256,896]{0,1:T(8,128)} %collective-permute-done.11), channel_id=1, source_target_pairs={{0,1},{1,0},{2,3},{3,2},{4,5},{5,4},{6,7},{7,6},{8,9},{9,8},{10,11... | collective-permute-start | bytes 2752520 | tf_op jit(solution)/shard_map/ppermute | solution.py:199
  112.1 60.3 %collective-permute-start.1 = (f32[1920,256]{1,0:T(8,128)}, f32[1920,256]{1,0:T(8,128)}, u32[]{:S(2)}, u32[]{:S(2)}) collective-permute-start(f32[1920,256]{1,0:T(8,128)} %get-tuple-element.74.own_ref), channel_id=1, source_target_pairs={{0,1},{1,0},{2,3},{3,2},{4,5},{5,4},{6,7},{7,6},{8,9},{9,8},{10,11... | collective-permute-start | bytes 5898248 | tf_op jit(solution)/shard_map/ppermute | solution.py:199
  112.6 28.4 %collective-permute-start.5 = (f32[256,896]{0,1:T(8,128)}, f32[256,896]{0,1:T(8,128)}, u32[]{:S(2)}, u32[]{:S(2)}) collective-permute-start(f32[256,896]{0,1:T(8,128)} %collective-permute-done.3), channel_id=1, source_target_pairs={{0,1},{1,0},{2,3},{3,2},{4,5},{5,4},{6,7},{7,6},{8,9},{9,8},{10,11... | collective-permute-start | bytes 2752520 | tf_op jit(solution)/shard_map/ppermute | solution.py:199
  126.4 46.5 %collective-permute-start.8 = (f32[1920,256]{1,0:T(8,128)}, f32[1920,256]{1,0:T(8,128)}, u32[]{:S(2)}, u32[]{:S(2)}) collective-permute-start(f32[1920,256]{1,0:T(8,128)} %get-tuple-element.80), channel_id=1, source_target_pairs={{0,4},{1,5},{2,6},{3,7},{4,0},{5,1},{6,2},{7,3},{8,12},{9,13},{10,... | collective-permute-start | bytes 5898248 | tf_op jit(solution)/shard_map/ppermute | solution.py:199
  127.0 59.8 %collective-permute-start.9 = (f32[1920,256]{1,0:T(8,128)}, f32[1920,256]{1,0:T(8,128)}, u32[]{:S(2)}, u32[]{:S(2)}) collective-permute-start(f32[1920,256]{1,0:T(8,128)} %get-tuple-element.79.own_ref), channel_id=1, source_target_pairs={{0,1},{1,0},{2,3},{3,2},{4,5},{5,4},{6,7},{7,6},{8,9},{9,8},{10,11... | collective-permute-start | bytes 5898248 | tf_op jit(solution)/shard_map/ppermute | solution.py:199
  140.9 59.2 %collective-permute-start.15 = (f32[1920,256]{1,0:T(8,128)}, f32[1920,256]{1,0:T(8,128)}, u32[]{:S(2)}, u32[]{:S(2)}) collective-permute-start(f32[1920,256]{1,0:T(8,128)} %get-tuple-element.85), channel_id=1, source_target_pairs={{0,2},{1,3},{2,0},{3,1},{4,6},{5,7},{6,4},{7,5},{8,10},{9,11},{10,... | collective-permute-start | bytes 5898248 | tf_op jit(solution)/shard_map/ppermute | solution.py:199
  157.9 56.3 %collective-permute-start.16 = (f32[1920,256]{1,0:T(8,128)}, f32[1920,256]{1,0:T(8,128)}, u32[]{:S(2)}, u32[]{:S(2)}) collective-permute-start(f32[1920,256]{1,0:T(8,128)} %get-tuple-element.84.own_ref), channel_id=1, source_target_pairs={{0,1},{1,0},{2,3},{3,2},{4,5},{5,4},{6,7},{7,6},{8,9},{9,8},{10,11... | collective-permute-start | bytes 5898248 | tf_op jit(solution)/shard_map/ppermute | solution.py:199
  172.3 44.8 %collective-permute-start.20 = (f32[1920,256]{1,0:T(8,128)}, f32[1920,256]{1,0:T(8,128)S(1)}, u32[]{:S(2)}, u32[]{:S(2)}) collective-permute-start(f32[1920,256]{1,0:T(8,128)} %get-tuple-element.90), channel_id=1, source_target_pairs={{0,4},{1,5},{2,6},{3,7},{4,0},{5,1},{6,2},{7,3},{8,12},{9,13},{10,... | collective-permute-start | bytes 5898248 | tf_op jit(solution)/shard_map/ppermute | solution.py:199
  172.9 58.8 %collective-permute-start.21 = (f32[1920,256]{1,0:T(8,128)}, f32[1920,256]{1,0:T(8,128)}, u32[]{:S(2)}, u32[]{:S(2)}) collective-permute-start(f32[1920,256]{1,0:T(8,128)} %get-tuple-element.89.own_ref), channel_id=1, source_target_pairs={{0,1},{1,0},{2,3},{3,2},{4,5},{5,4},{6,7},{7,6},{8,9},{9,8},{10,11... | collective-permute-start | bytes 5898248 | tf_op jit(solution)/shard_map/ppermute | solution.py:199
  186.8 55.4 %collective-permute-start.25 = (f32[1920,256]{1,0:T(8,128)}, f32[1920,256]{1,0:T(8,128)}, u32[]{:S(2)}, u32[]{:S(2)}) collective-permute-start(f32[1920,256]{1,0:T(8,128)} %get-tuple-element.95), channel_id=1, source_target_pairs={{0,2},{1,3},{2,0},{3,1},{4,6},{5,7},{6,4},{7,5},{8,10},{9,11},{10,... | collective-permute-start | bytes 5898248 | tf_op jit(solution)/shard_map/ppermute | solution.py:199
  200.1 55.9 %collective-permute-start.26 = (f32[1920,256]{1,0:T(8,128)}, f32[1920,256]{1,0:T(8,128)}, u32[]{:S(2)}, u32[]{:S(2)}) collective-permute-start(f32[1920,256]{1,0:T(8,128)} %get-tuple-element.94.own_ref), channel_id=1, source_target_pairs={{0,1},{1,0},{2,3},{3,2},{4,5},{5,4},{6,7},{7,6},{8,9},{9,8},{10,11... | collective-permute-start | bytes 5898248 | tf_op jit(solution)/shard_map/ppermute | solution.py:199
  214.1 45.8 %collective-permute-start.30 = (f32[1920,256]{1,0:T(8,128)}, f32[1920,256]{1,0:T(8,128)}, u32[]{:S(2)}, u32[]{:S(2)}) collective-permute-start(f32[1920,256]{1,0:T(8,128)} %get-tuple-element.100), channel_id=1, source_target_pairs={{0,4},{1,5},{2,6},{3,7},{4,0},{5,1},{6,2},{7,3},{8,12},{9,13},{10,... | collective-permute-start | bytes 5898248 | tf_op jit(solution)/shard_map/ppermute | solution.py:199
  217.1 56.6 %collective-permute-start.31 = (f32[1920,256]{1,0:T(8,128)}, f32[1920,256]{1,0:T(8,128)}, u32[]{:S(2)}, u32[]{:S(2)}) collective-permute-start(f32[1920,256]{1,0:T(8,128)} %get-tuple-element.99.own_ref), channel_id=1, source_target_pairs={{0,1},{1,0},{2,3},{3,2},{4,5},{5,4},{6,7},{7,6},{8,9},{9,8},{10,11... | collective-permute-start | bytes 5898248 | tf_op jit(solution)/shard_map/ppermute | solution.py:199
  231.7 52.7 %collective-permute-start.35 = (f32[1920,256]{1,0:T(8,128)}, f32[1920,256]{1,0:T(8,128)}, u32[]{:S(2)}, u32[]{:S(2)}) collective-permute-start(f32[1920,256]{1,0:T(8,128)} %get-tuple-element.105), channel_id=1, source_target_pairs={{0,2},{1,3},{2,0},{3,1},{4,6},{5,7},{6,4},{7,5},{8,10},{9,11},{10,... | collective-permute-start | bytes 5898248 | tf_op jit(solution)/shard_map/ppermute | solution.py:199
  242.2 56.3 %collective-permute-start.36 = (f32[1920,256]{1,0:T(8,128)}, f32[1920,256]{1,0:T(8,128)}, u32[]{:S(2)}, u32[]{:S(2)}) collective-permute-start(f32[1920,256]{1,0:T(8,128)} %get-tuple-element.104.own_ref), channel_id=1, source_target_pairs={{0,1},{1,0},{2,3},{3,2},{4,5},{5,4},{6,7},{7,6},{8,9},{9,8},{10,11... | collective-permute-start | bytes 5898248 | tf_op jit(solution)/shard_map/ppermute | solution.py:199
  256.0 45.8 %collective-permute-start.40 = (f32[1920,256]{1,0:T(8,128)}, f32[1920,256]{1,0:T(8,128)}, u32[]{:S(2)}, u32[]{:S(2)}) collective-permute-start(f32[1920,256]{1,0:T(8,128)} %get-tuple-element.110), channel_id=1, source_target_pairs={{0,4},{1,5},{2,6},{3,7},{4,0},{5,1},{6,2},{7,3},{8,12},{9,13},{10,... | collective-permute-start | bytes 5898248 | tf_op jit(solution)/shard_map/ppermute | solution.py:199
  259.9 44.3 %collective-permute-start.41 = (f32[1920,256]{1,0:T(8,128)}, f32[1920,256]{1,0:T(8,128)}, u32[]{:S(2)}, u32[]{:S(2)}) collective-permute-start(f32[1920,256]{1,0:T(8,128)} %get-tuple-element.109.own_ref), channel_id=1, source_target_pairs={{0,1},{1,0},{2,3},{3,2},{4,5},{5,4},{6,7},{7,6},{8,9},{9,8},{10,11... | collective-permute-start | bytes 5898248 | tf_op jit(solution)/shard_map/ppermute | solution.py:199
  273.7 51.6 %collective-permute-start.45 = (f32[1920,256]{1,0:T(8,128)}, f32[1920,256]{1,0:T(8,128)}, u32[]{:S(2)}, u32[]{:S(2)}) collective-permute-start(f32[1920,256]{1,0:T(8,128)} %get-tuple-element.115), channel_id=1, source_target_pairs={{0,2},{1,3},{2,0},{3,1},{4,6},{5,7},{6,4},{7,5},{8,10},{9,11},{10,... | collective-permute-start | bytes 5898248 | tf_op jit(solution)/shard_map/ppermute | solution.py:199
  284.4 68.8 %collective-permute-start.46 = (f32[1920,256]{1,0:T(8,128)}, f32[1920,256]{1,0:T(8,128)}, u32[]{:S(2)}, u32[]{:S(2)}) collective-permute-start(f32[1920,256]{1,0:T(8,128)} %get-tuple-element.114.own_ref), channel_id=1, source_target_pairs={{0,1},{1,0},{2,3},{3,2},{4,5},{5,4},{6,7},{7,6},{8,9},{9,8},{10,11... | collective-permute-start | bytes 5898248 | tf_op jit(solution)/shard_map/ppermute | solution.py:199
  298.5 53.1 %copy-start.3 = (bf16[256,896]{0,1:T(8,128)(2,1)S(1)}, bf16[256,896]{0,1:T(8,128)(2,1)}, u32[]{:S(2)}) copy-start(bf16[256,896]{0,1:T(8,128)(2,1)} %copy-done.2) | copy-start | bytes 1376260
  298.5 53.1 %copy-start.45 = (f32[896]{0:T(1024)S(1)}, f32[896]{0:T(1024)}, u32[]{:S(2)}) copy-start(f32[896]{0:T(1024)} %copy-done.44) | copy-start | bytes 10756
  298.5 53.0 %copy-start.47 = (f32[256]{0:T(256)S(1)}, f32[256]{0:T(256)}, u32[]{:S(2)}) copy-start(f32[256]{0:T(256)} %copy-done.46) | copy-start | bytes 3076
  298.5 54.7 %collective-permute-start.50 = (f32[1920,256]{1,0:T(8,128)}, f32[1920,256]{1,0:T(8,128)}, u32[]{:S(2)}, u32[]{:S(2)}) collective-permute-start(f32[1920,256]{1,0:T(8,128)} %get-tuple-element.120), channel_id=1, source_target_pairs={{0,4},{1,5},{2,6},{3,7},{4,0},{5,1},{6,2},{7,3},{8,12},{9,13},{10,... | collective-permute-start | bytes 5898248 | tf_op jit(solution)/shard_map/ppermute | solution.py:199
  301.8 71.1 %collective-permute-start.51 = (f32[1920,256]{1,0:T(8,128)}, f32[1920,256]{1,0:T(8,128)}, u32[]{:S(2)}, u32[]{:S(2)}) collective-permute-start(f32[1920,256]{1,0:T(8,128)} %get-tuple-element.119.own_ref), channel_id=1, source_target_pairs={{0,1},{1,0},{2,3},{3,2},{4,5},{5,4},{6,7},{7,6},{8,9},{9,8},{10,11... | collective-permute-start | bytes 5898248 | tf_op jit(solution)/shard_map/ppermute | solution.py:199
  301.8 51.4 %copy-start.49 = (f32[256]{0:T(256)S(1)}, f32[256]{0:T(256)}, u32[]{:S(2)}) copy-start(f32[256]{0:T(256)} %copy-done.48) | copy-start | bytes 3076
  304.3 71.9 %collective-permute-start.2 = (f32[1920,256]{1,0:T(8,128)S(1)}, f32[1920,256]{1,0:T(8,128)}, u32[]{:S(2)}, u32[]{:S(2)}) collective-permute-start(f32[1920,256]{1,0:T(8,128)S(1)} %copy-done.26), channel_id=1, source_target_pairs={{0,1},{1,0},{2,3},{3,2},{4,5},{5,4},{6,7},{7,6},{8,9},{9,8},{10,11... | collective-permute-start | bytes 5898248 | tf_op jit(solution)/shard_map/ppermute | solution.py:199
  325.4 51.9 %collective-permute-start.10 = (f32[1920,256]{1,0:T(8,128)}, f32[1920,256]{1,0:T(8,128)}, u32[]{:S(2)}, u32[]{:S(2)}) collective-permute-start(f32[1920,256]{1,0:T(8,128)} %collective-permute-done.8.near_ref), channel_id=1, source_target_pairs={{0,1},{1,0},{2,3},{3,2},{4,5},{5,4},{6,7},{7,6},{8,9},{9,8},{10,11... | collective-permute-start | bytes 5898248 | tf_op jit(solution)/shard_map/ppermute | solution.py:199
  325.4 47.5 %copy-start.14 = (f32[256,896]{0,1:T(8,128)S(1)}, f32[256,896]{0,1:T(8,128)}, u32[]{:S(2)}) copy-start(f32[256,896]{0,1:T(8,128)} %copy-done.13) | copy-start | bytes 2752516
  353.1 26.4 %collective-permute-start.17 = (f32[1920,256]{1,0:T(8,128)}, f32[1920,256]{1,0:T(8,128)}, u32[]{:S(2)}, u32[]{:S(2)}) collective-permute-start(f32[1920,256]{1,0:T(8,128)} %collective-permute-done.15.near_ref), channel_id=1, source_target_pairs={{0,1},{1,0},{2,3},{3,2},{4,5},{5,4},{6,7},{7,6},{8,9},{9,8},{10,11... | collective-permute-start | bytes 5898248 | tf_op jit(solution)/shard_map/ppermute | solution.py:199
  353.3 27.0 %collective-permute-start.22 = (f32[1920,256]{1,0:T(8,128)}, f32[1920,256]{1,0:T(8,128)}, u32[]{:S(2)}, u32[]{:S(2)}) collective-permute-start(f32[1920,256]{1,0:T(8,128)} %copy-done.27), channel_id=1, source_target_pairs={{0,1},{1,0},{2,3},{3,2},{4,5},{5,4},{6,7},{7,6},{8,9},{9,8},{10,11... | collective-permute-start | bytes 5898248 | tf_op jit(solution)/shard_map/ppermute | solution.py:199
  372.9 11.9 %collective-permute-start.27 = (f32[1920,256]{1,0:T(8,128)}, f32[1920,256]{1,0:T(8,128)}, u32[]{:S(2)}, u32[]{:S(2)}) collective-permute-start(f32[1920,256]{1,0:T(8,128)} %collective-permute-done.25.near_ref), channel_id=1, source_target_pairs={{0,1},{1,0},{2,3},{3,2},{4,5},{5,4},{6,7},{7,6},{8,9},{9,8},{10,11... | collective-permute-start | bytes 5898248 | tf_op jit(solution)/shard_map/ppermute | solution.py:199
  376.2 18.8 %collective-permute-start.32 = (f32[1920,256]{1,0:T(8,128)}, f32[1920,256]{1,0:T(8,128)}, u32[]{:S(2)}, u32[]{:S(2)}) collective-permute-start(f32[1920,256]{1,0:T(8,128)} %collective-permute-done.30.near_ref), channel_id=1, source_target_pairs={{0,1},{1,0},{2,3},{3,2},{4,5},{5,4},{6,7},{7,6},{8,9},{9,8},{10,11... | collective-permute-start | bytes 5898248 | tf_op jit(solution)/shard_map/ppermute | solution.py:199
  377.2 30.2 %collective-permute-start.37 = (f32[1920,256]{1,0:T(8,128)}, f32[1920,256]{1,0:T(8,128)}, u32[]{:S(2)}, u32[]{:S(2)}) collective-permute-start(f32[1920,256]{1,0:T(8,128)} %collective-permute-done.35.near_ref), channel_id=1, source_target_pairs={{0,1},{1,0},{2,3},{3,2},{4,5},{5,4},{6,7},{7,6},{8,9},{9,8},{10,11... | collective-permute-start | bytes 5898248 | tf_op jit(solution)/shard_map/ppermute | solution.py:199
  379.6 51.7 %collective-permute-start.42 = (f32[1920,256]{1,0:T(8,128)}, f32[1920,256]{1,0:T(8,128)}, u32[]{:S(2)}, u32[]{:S(2)}) collective-permute-start(f32[1920,256]{1,0:T(8,128)} %collective-permute-done.40.near_ref), channel_id=1, source_target_pairs={{0,1},{1,0},{2,3},{3,2},{4,5},{5,4},{6,7},{7,6},{8,9},{9,8},{10,11... | collective-permute-start | bytes 5898248 | tf_op jit(solution)/shard_map/ppermute | solution.py:199
  380.3 76.2 %collective-permute-start.47 = (f32[1920,256]{1,0:T(8,128)}, f32[1920,256]{1,0:T(8,128)}, u32[]{:S(2)}, u32[]{:S(2)}) collective-permute-start(f32[1920,256]{1,0:T(8,128)} %collective-permute-done.45.near_ref), channel_id=1, source_target_pairs={{0,1},{1,0},{2,3},{3,2},{4,5},{5,4},{6,7},{7,6},{8,9},{9,8},{10,11... | collective-permute-start | bytes 5898248 | tf_op jit(solution)/shard_map/ppermute | solution.py:199
  384.9 81.7 %collective-permute-start.52 = (f32[1920,256]{1,0:T(8,128)}, f32[1920,256]{1,0:T(8,128)}, u32[]{:S(2)}, u32[]{:S(2)}) collective-permute-start(f32[1920,256]{1,0:T(8,128)} %collective-permute-done.50.near_ref), channel_id=1, source_target_pairs={{0,1},{1,0},{2,3},{3,2},{4,5},{5,4},{6,7},{7,6},{8,9},{9,8},{10,11... | collective-permute-start | bytes 5898248 | tf_op jit(solution)/shard_map/ppermute | solution.py:199
  395.0 80.4 %collective-permute-start.6 = (f32[224,1920]{1,0:T(8,128)}, f32[224,1920]{1,0:T(8,128)S(1)}, u32[]{:S(2)}, u32[]{:S(2)}) collective-permute-start(f32[224,1920]{1,0:T(8,128)} %get-tuple-element.77), channel_id=1, source_target_pairs={{0,4},{1,5},{2,6},{3,7},{4,0},{5,1},{6,2},{7,3},{8,12},{9,13},{10,... | collective-permute-start | bytes 5160968 | tf_op jit(solution)/shard_map/ppermute | solution.py:199
  407.4 69.4 %collective-permute-start.13 = (f32[224,1920]{1,0:T(8,128)}, f32[224,1920]{1,0:T(8,128)S(1)}, u32[]{:S(2)}, u32[]{:S(2)}) collective-permute-start(f32[224,1920]{1,0:T(8,128)} %get-tuple-element.82), channel_id=1, source_target_pairs={{0,2},{1,3},{2,0},{3,1},{4,6},{5,7},{6,4},{7,5},{8,10},{9,11},{10,... | collective-permute-start | bytes 5160968 | tf_op jit(solution)/shard_map/ppermute | solution.py:199
  431.2 48.3 %collective-permute-start.18 = (f32[224,1920]{1,0:T(8,128)}, f32[224,1920]{1,0:T(8,128)}, u32[]{:S(2)}, u32[]{:S(2)}) collective-permute-start(f32[224,1920]{1,0:T(8,128)} %get-tuple-element.87), channel_id=1, source_target_pairs={{0,4},{1,5},{2,6},{3,7},{4,0},{5,1},{6,2},{7,3},{8,12},{9,13},{10,... | collective-permute-start | bytes 5160968 | tf_op jit(solution)/shard_map/ppermute | solution.py:199
  456.5 40.8 %collective-permute-start.23 = (f32[224,1920]{1,0:T(8,128)}, f32[224,1920]{1,0:T(8,128)}, u32[]{:S(2)}, u32[]{:S(2)}) collective-permute-start(f32[224,1920]{1,0:T(8,128)} %get-tuple-element.92), channel_id=1, source_target_pairs={{0,2},{1,3},{2,0},{3,1},{4,6},{5,7},{6,4},{7,5},{8,10},{9,11},{10,... | collective-permute-start | bytes 5160968 | tf_op jit(solution)/shard_map/ppermute | solution.py:199
  466.5 43.0 %collective-permute-start.28 = (f32[224,1920]{1,0:T(8,128)}, f32[224,1920]{1,0:T(8,128)}, u32[]{:S(2)}, u32[]{:S(2)}) collective-permute-start(f32[224,1920]{1,0:T(8,128)} %get-tuple-element.97), channel_id=1, source_target_pairs={{0,4},{1,5},{2,6},{3,7},{4,0},{5,1},{6,2},{7,3},{8,12},{9,13},{10,... | collective-permute-start | bytes 5160968 | tf_op jit(solution)/shard_map/ppermute | solution.py:199
  475.3 58.8 %collective-permute-start.33 = (f32[224,1920]{1,0:T(8,128)}, f32[224,1920]{1,0:T(8,128)S(1)}, u32[]{:S(2)}, u32[]{:S(2)}) collective-permute-start(f32[224,1920]{1,0:T(8,128)} %get-tuple-element.102), channel_id=1, source_target_pairs={{0,2},{1,3},{2,0},{3,1},{4,6},{5,7},{6,4},{7,5},{8,10},{9,11},{10,... | collective-permute-start | bytes 5160968 | tf_op jit(solution)/shard_map/ppermute | solution.py:199
  477.0 69.2 %collective-permute-start.38 = (f32[224,1920]{1,0:T(8,128)S(1)}, f32[224,1920]{1,0:T(8,128)S(1)}, u32[]{:S(2)}, u32[]{:S(2)}) collective-permute-start(f32[224,1920]{1,0:T(8,128)S(1)} %copy-done.52), channel_id=1, source_target_pairs={{0,4},{1,5},{2,6},{3,7},{4,0},{5,1},{6,2},{7,3},{8,12},{9,13},{10,... | collective-permute-start | bytes 5160968 | tf_op jit(solution)/shard_map/ppermute | solution.py:199
  479.5 91.5 %collective-permute-start.43 = (f32[224,1920]{1,0:T(8,128)S(1)}, f32[224,1920]{1,0:T(8,128)S(1)}, u32[]{:S(2)}, u32[]{:S(2)}) collective-permute-start(f32[224,1920]{1,0:T(8,128)S(1)} %copy-done.51), channel_id=1, source_target_pairs={{0,2},{1,3},{2,0},{3,1},{4,6},{5,7},{6,4},{7,5},{8,10},{9,11},{10,... | collective-permute-start | bytes 5160968 | tf_op jit(solution)/shard_map/ppermute | solution.py:199
  497.3 85.8 %collective-permute-start.48 = (f32[224,1920]{1,0:T(8,128)S(1)}, f32[224,1920]{1,0:T(8,128)S(1)}, u32[]{:S(2)}, u32[]{:S(2)}) collective-permute-start(f32[224,1920]{1,0:T(8,128)S(1)} %copy-done.53), channel_id=1, source_target_pairs={{0,4},{1,5},{2,6},{3,7},{4,0},{5,1},{6,2},{7,3},{8,12},{9,13},{10,... | collective-permute-start | bytes 5160968 | tf_op jit(solution)/shard_map/ppermute | solution.py:199
  509.5 98.3 %collective-permute-start.53 = (f32[224,1920]{1,0:T(8,128)S(1)}, f32[224,1920]{1,0:T(8,128)S(1)}, u32[]{:S(2)}, u32[]{:S(2)}) collective-permute-start(f32[224,1920]{1,0:T(8,128)S(1)} %copy-done.54), channel_id=1, source_target_pairs={{0,2},{1,3},{2,0},{3,1},{4,6},{5,7},{6,4},{7,5},{8,10},{9,11},{10,... | collective-permute-start | bytes 5160968 | tf_op jit(solution)/shard_map/ppermute | solution.py:199
  534.1 92.2 %collective-permute-start.7 = (f32[112,1920]{1,0:T(8,128)S(1)}, f32[112,1920]{1,0:T(8,128)S(1)}, u32[]{:S(2)}, u32[]{:S(2)}) collective-permute-start(f32[112,1920]{1,0:T(8,128)S(1)} %slice_add_fusion.18), channel_id=1, source_target_pairs={{0,2},{1,3},{2,0},{3,1},{4,6},{5,7},{6,4},{7,5},{8,10},{9,11},{10,... | collective-permute-start | bytes 2580488 | tf_op jit(solution)/shard_map/ppermute | solution.py:199
  546.3 86.0 %collective-permute-start.14 = (f32[112,1920]{1,0:T(8,128)}, f32[112,1920]{1,0:T(8,128)}, u32[]{:S(2)}, u32[]{:S(2)}) collective-permute-start(f32[112,1920]{1,0:T(8,128)} %slice_add_fusion.16), channel_id=1, source_target_pairs={{0,4},{1,5},{2,6},{3,7},{4,0},{5,1},{6,2},{7,3},{8,12},{9,13},{10,... | collective-permute-start | bytes 2580488 | tf_op jit(solution)/shard_map/ppermute | solution.py:199
  571.0 73.8 %collective-permute-start.19 = (f32[112,1920]{1,0:T(8,128)}, f32[112,1920]{1,0:T(8,128)}, u32[]{:S(2)}, u32[]{:S(2)}) collective-permute-start(f32[112,1920]{1,0:T(8,128)} %slice_add_fusion.14), channel_id=1, source_target_pairs={{0,2},{1,3},{2,0},{3,1},{4,6},{5,7},{6,4},{7,5},{8,10},{9,11},{10,... | collective-permute-start | bytes 2580488 | tf_op jit(solution)/shard_map/ppermute | solution.py:199
  583.1 65.2 %collective-permute-start.24 = (f32[112,1920]{1,0:T(8,128)}, f32[112,1920]{1,0:T(8,128)}, u32[]{:S(2)}, u32[]{:S(2)}) collective-permute-start(f32[112,1920]{1,0:T(8,128)} %slice_add_fusion.12), channel_id=1, source_target_pairs={{0,4},{1,5},{2,6},{3,7},{4,0},{5,1},{6,2},{7,3},{8,12},{9,13},{10,... | collective-permute-start | bytes 2580488 | tf_op jit(solution)/shard_map/ppermute | solution.py:199
  584.0 43.2 %copy-start.21 = (f32[112,1920]{1,0:T(8,128)S(1)}, f32[112,1920]{1,0:T(8,128)}, u32[]{:S(2)}) copy-start(f32[112,1920]{1,0:T(8,128)} %get-tuple-element.76) | copy-start | bytes 2580484
  607.8 55.4 %collective-permute-start.29 = (f32[112,1920]{1,0:T(8,128)}, f32[112,1920]{1,0:T(8,128)}, u32[]{:S(2)}, u32[]{:S(2)}) collective-permute-start(f32[112,1920]{1,0:T(8,128)} %slice_add_fusion.10), channel_id=1, source_target_pairs={{0,2},{1,3},{2,0},{3,1},{4,6},{5,7},{6,4},{7,5},{8,10},{9,11},{10,... | collective-permute-start | bytes 2580488 | tf_op jit(solution)/shard_map/ppermute | solution.py:199
  626.3 40.5 %collective-permute-start.34 = (f32[112,1920]{1,0:T(8,128)}, f32[112,1920]{1,0:T(8,128)}, u32[]{:S(2)}, u32[]{:S(2)}) collective-permute-start(f32[112,1920]{1,0:T(8,128)} %slice_add_fusion.8), channel_id=1, source_target_pairs={{0,4},{1,5},{2,6},{3,7},{4,0},{5,1},{6,2},{7,3},{8,12},{9,13},{10,... | collective-permute-start | bytes 2580488 | tf_op jit(solution)/shard_map/ppermute | solution.py:199
  632.3 49.3 %collective-permute-start.39 = (f32[112,1920]{1,0:T(8,128)S(1)}, f32[112,1920]{1,0:T(8,128)S(1)}, u32[]{:S(2)}, u32[]{:S(2)}) collective-permute-start(f32[112,1920]{1,0:T(8,128)S(1)} %copy-done.33), channel_id=1, source_target_pairs={{0,2},{1,3},{2,0},{3,1},{4,6},{5,7},{6,4},{7,5},{8,10},{9,11},{10,... | collective-permute-start | bytes 2580488 | tf_op jit(solution)/shard_map/ppermute | solution.py:199
  644.8 37.2 %collective-permute-start.44 = (f32[112,1920]{1,0:T(8,128)S(1)}, f32[112,1920]{1,0:T(8,128)S(1)}, u32[]{:S(2)}, u32[]{:S(2)}) collective-permute-start(f32[112,1920]{1,0:T(8,128)S(1)} %copy-done.32), channel_id=1, source_target_pairs={{0,4},{1,5},{2,6},{3,7},{4,0},{5,1},{6,2},{7,3},{8,12},{9,13},{10,... | collective-permute-start | bytes 2580488 | tf_op jit(solution)/shard_map/ppermute | solution.py:199
  648.4 50.6 %collective-permute-start.49 = (f32[112,1920]{1,0:T(8,128)S(1)}, f32[112,1920]{1,0:T(8,128)S(1)}, u32[]{:S(2)}, u32[]{:S(2)}) collective-permute-start(f32[112,1920]{1,0:T(8,128)S(1)} %copy-done.31), channel_id=1, source_target_pairs={{0,2},{1,3},{2,0},{3,1},{4,6},{5,7},{6,4},{7,5},{8,10},{9,11},{10,... | collective-permute-start | bytes 2580488 | tf_op jit(solution)/shard_map/ppermute | solution.py:199
  663.2 36.1 %collective-permute-start.54 = (f32[112,1920]{1,0:T(8,128)S(1)}, f32[112,1920]{1,0:T(8,128)S(1)}, u32[]{:S(2)}, u32[]{:S(2)}) collective-permute-start(f32[112,1920]{1,0:T(8,128)S(1)} %copy-done.30), channel_id=1, source_target_pairs={{0,4},{1,5},{2,6},{3,7},{4,0},{5,1},{6,2},{7,3},{8,12},{9,13},{10,... | collective-permute-start | bytes 2580488 | tf_op jit(solution)/shard_map/ppermute | solution.py:199
  (47 other events, 584.2 us)
Sparse Core Ops, SparseCore 0:
  304.4 47.0 all-reduce.3

commit v2 on v1

--- a/solution.py
+++ b/solution.py
@@ -12,6 +12,7 @@
 LOG2E = 1.4426950408889634
 CAP2 = SOFT_CAP * LOG2E
 CHUNKS = 10
+EARLY = 4
 HALF = 1920
 ROWS_F = 1024
 ROWS_B = 960
@@ -85,20 +86,25 @@
     )(emb, teach_t, g_t)
 
 
-def grad_kernel(limit, first, nb, side_ref, e_ref, t_ref, g_ref, st_ref, acc_ref, send_ref, own_ref, dg_ref):
-    h, j = pl.program_id(0), pl.program_id(1)
-    rows = e_ref.shape[0]
-
-    @pl.when((h == 0) & (j == 0))
-    def _():
-        dg_ref[...] = acc_ref[...]
-
-    emb = e_ref[...]
+def logit_grad(emb, t, g_ref, st_ref):
     raw = jnp.dot(emb, g_ref[...], preferred_element_type=jnp.float32)
     u = jnp.tanh(raw * (1.0 / SOFT_CAP))
     ez = jnp.exp2(u * CAP2 - CAP2)
-    et = jnp.exp2((t_ref[...].astype(jnp.float32) - st_ref[1:2, :]) * LOG2E)
-    dr = (ez * st_ref[0:1, :] - et * st_ref[2:3, :]) * (1.0 - u * u)
+    et = jnp.exp2((t.astype(jnp.float32) - st_ref[1:2, :]) * LOG2E)
+    return (ez * st_ref[0:1, :] - et * st_ref[2:3, :]) * (1.0 - u * u)
+
+
+def grad_kernel(limit, first, nb, side_ref, e_ref, t_ref, g_ref, st_ref, acc_ref, *out_refs):
+    *send_refs, own_ref, dg_ref = out_refs
+    h, j = pl.program_id(0), pl.program_id(1)
+    rows = e_ref.shape[0]
+
+    @pl.when((h == 0) & (j == 0))
+    def _():
+        dg_ref[...] = acc_ref[...]
+
+    emb = e_ref[...]
+    dr = logit_grad(emb, t_ref[...], g_ref, st_ref)
     if limit is not None:
         half = jnp.where(h == 0, 1 - side_ref[0], side_ref[0])
         left = limit - (first + half * nb + j) * rows
@@ -107,9 +113,11 @@
     dr = dr.astype(jnp.bfloat16)
     wide = dr.astype(jnp.float32)
 
-    @pl.when(h == 0)
-    def _():
-        send_ref[...] = wide
+    for send_ref in send_refs:
+
+        @pl.when(h == 0)
+        def _():
+            send_ref[...] = wide
 
     @pl.when(h == 1)
     def _():
@@ -118,7 +126,7 @@
     dg_ref[...] += lax.dot_general(dr, emb, (((0,), (0,)), ((), ())), preferred_element_type=jnp.float32)
 
 
-def chunk_grad(chunk, side, emb, teach_t, g_t, stats, acc):
+def chunk_grad(chunk, send, side, emb, teach_t, g_t, stats, acc):
     vocab, dim = emb.shape
     tok = teach_t.shape[1]
     nb = HALF // ROWS_B
@@ -133,7 +141,7 @@
     half_shape = jax.ShapeDtypeStruct((HALF, tok), jnp.float32)
     return pl.pallas_call(
         functools.partial(grad_kernel, limit, first, nb),
-        out_shape=(half_shape, half_shape, jax.ShapeDtypeStruct((tok, dim), jnp.float32)),
+        out_shape=(half_shape,) * (2 if send else 1) + (jax.ShapeDtypeStruct((tok, dim), jnp.float32),),
         grid_spec=pltpu.PrefetchScalarGridSpec(
             num_scalar_prefetch=1,
             grid=(2, nb),
@@ -144,17 +152,102 @@
                 pl.BlockSpec((8, tok), whole),
                 pl.BlockSpec((tok, dim), whole),
             ],
-            out_specs=(
-                pl.BlockSpec((ROWS_B, tok), lambda h, j, s: (jnp.where(h == 0, j, nb - 1), 0)),
+            out_specs=([pl.BlockSpec((ROWS_B, tok), lambda h, j, s: (jnp.where(h == 0, j, nb - 1), 0))] if send else [])
+            + [
                 pl.BlockSpec((ROWS_B, tok), lambda h, j, s: (jnp.where(h == 0, 0, j), 0)),
                 pl.BlockSpec((tok, dim), whole),
-            ),
+            ],
         ),
         cost_estimate=pl.CostEstimate(
             flops=8 * HALF * dim * tok, bytes_accessed=4 * HALF * (dim + 3 * tok), transcendentals=6 * HALF * tok
         ),
         name="grad",
     )(side, emb, teach_t, g_t, stats, acc)
+
+
+def near_kernel(side_ref, e_ref, t_ref, g_ref, st_ref, out_ref):
+    dr = logit_grad(e_ref[...], t_ref[...], g_ref, st_ref)
+    out_ref[...] = dr.astype(jnp.bfloat16).astype(jnp.float32)
+
+
+def near_grad(chunk, side, emb, teach_near, g_t, stats):
+    rows, tok = teach_near.shape
+    dim = emb.shape[1]
+    nb = rows // ROWS_B
+    whole = lambda j, side_ref: (0, 0)
+    return pl.pallas_call(
+        near_kernel,
+        out_shape=jax.ShapeDtypeStruct((rows, tok), jnp.float32),
+        grid_spec=pltpu.PrefetchScalarGridSpec(
+            num_scalar_prefetch=1,
+            grid=(nb,),
+            in_specs=[
+                pl.BlockSpec((ROWS_B, dim), lambda j, side_ref: ((2 * chunk + side_ref[0]) * nb + j, 0)),
+                pl.BlockSpec((ROWS_B, tok), lambda j, side_ref: (j, 0)),
+                pl.BlockSpec((dim, tok), whole),
+                pl.BlockSpec((8, tok), whole),
+            ],
+            out_specs=pl.BlockSpec((ROWS_B, tok), lambda j, side_ref: (j, 0)),
+        ),
+        cost_estimate=pl.CostEstimate(
+            flops=2 * rows * dim * tok, bytes_accessed=2 * rows * (dim + 4 * tok), transcendentals=3 * rows * tok
+        ),
+        name="near",
+    )(side, emb, teach_near, g_t, stats)
+
+
+def widen_kernel(side_ref, t_ref, out_ref):
+    out_ref[...] = t_ref[...].astype(jnp.float32)
+
+
+def widen_half(chunk, side, teach_t):
+    tok = teach_t.shape[1]
+    nb = HALF // ROWS_B
+    return pl.pallas_call(
+        widen_kernel,
+        out_shape=jax.ShapeDtypeStruct((HALF, tok), jnp.float32),
+        grid_spec=pltpu.PrefetchScalarGridSpec(
+            num_scalar_prefetch=1,
+            grid=(nb,),
+            in_specs=[pl.BlockSpec((ROWS_B, tok), lambda j, side_ref: ((2 * chunk + 1 - side_ref[0]) * nb + j, 0))],
+            out_specs=pl.BlockSpec((ROWS_B, tok), lambda j, side_ref: (j, 0)),
+        ),
+        cost_estimate=pl.CostEstimate(flops=HALF * tok, bytes_accessed=6 * HALF * tok, transcendentals=0),
+        name="widen",
+    )(side, teach_t)
+
+
+def place_kernel(side_ref, mine_ref, other_ref, *refs):
+    out_ref = refs[-1]
+
+    @pl.when(pl.program_id(0) == 0)
+    def _():
+        out_ref[...] = mine_ref[...]
+
+    @pl.when(pl.program_id(0) == 1)
+    def _():
+        out_ref[...] = other_ref[...]
+
+
+def place(chunk, side, mine, other, vocab, out):
+    cols, rows = mine.shape
+    whole = lambda h, side_ref: (0, 0)
+    given = [] if out is None else [out]
+    return pl.pallas_call(
+        place_kernel,
+        out_shape=jax.ShapeDtypeStruct((cols, vocab), jnp.float32),
+        grid_spec=pltpu.PrefetchScalarGridSpec(
+            num_scalar_prefetch=1,
+            grid=(2,),
+            in_specs=[pl.BlockSpec((cols, rows), whole)] * 2 + [pl.BlockSpec(memory_space=pl.ANY)] * len(given),
+            out_specs=pl.BlockSpec(
+                (cols, rows), lambda h, side_ref: (0, 2 * chunk + jnp.where(h == 0, side_ref[0], 1 - side_ref[0]))
+            ),
+        ),
+        input_output_aliases={3: 0} if given else {},
+        cost_estimate=pl.CostEstimate(flops=cols * rows, bytes_accessed=16 * cols * rows, transcendentals=0),
+        name="place",
+    )(side, mine, other, *given)
 
 
 def table_kernel(own_ref, near_ref, core_ref, far_ref, g_ref, send_ref, keep_ref, pass_ref, held):
@@ -192,18 +285,43 @@
 
 
 def solution(mesh):
-    dp = mesh.shape['dp']
+    dp, tp = mesh.shape['dp'], mesh.shape['tp']
     bits = {'core': 1, 'x': 2, 'y': 4}
 
-    def swap(a, axis):
-        return lax.ppermute(a, 'dp', [(i, i ^ bits[axis]) for i in range(dp)])
+    def trade(a, axis, mask):
+        size = mesh.shape[axis]
+        return lax.ppermute(a, axis, [(i, i ^ mask) for i in range(size)])
+
+    def swap(a, link):
+        return trade(a, 'dp', bits[link])
+
+    def tree(parts, join):
+        while len(parts) > 1:
+            parts = [join(parts[i], parts[i + 1]) for i in range(0, len(parts), 2)]
+        return parts[0]
+
+    def join_stats(one, two):
+        top = jnp.maximum(one[1], two[1])
+        first, second = jnp.exp(one[1] - top), jnp.exp(two[1] - top)
+        return (
+            one[0] + two[0],
+            top,
+            one[2] * first + two[2] * second,
+            one[3] * first + two[3] * second,
+        )
+
+    late = list(range(EARLY, CHUNKS))
+    early = list(range(EARLY))
+    axes = [('x', 'y') if chunk % 2 == 0 else ('y', 'x') for chunk in range(CHUNKS)]
 
     def device_fn(hid_loc, norm_w, emb_loc, teach_loc, mask_loc):
         vocab, dim = emb_loc.shape
         me = lax.axis_index('dp')
-        place = {axis: (me // bit) % 2 for axis, bit in bits.items()}
+        place_of = {axis: (me // bit) % 2 for axis, bit in bits.items()}
+        side = {axis: place_of[axis].astype(jnp.int32)[None] for axis in 'xy'}
         mask_f32 = mask_loc.astype(jnp.float32)
-        tok_count = lax.psum(jnp.sum(mask_f32), 'dp')
+        own_count = jnp.full((8, 128), jnp.sum(mask_f32))
+        tok_count = tree([own_count] + [trade(own_count, 'dp', k) for k in range(1, dp)], jnp.add)[0, 0]
         weight = mask_f32 / tok_count
         normed_f32, norm_pull = jax.vjp(rms_norm, hid_loc.astype(jnp.float32), norm_w.astype(jnp.float32))
         normed = lax.optimization_barrier(normed_f32.astype(jnp.bfloat16))
@@ -213,13 +331,18 @@
         g_own = normed.astype(jnp.float32)
         near = {axis: swap(g_own, axis) for axis in 'xy'}
         g_core = swap(g_own, 'core')
+        teach_near = []
+        for chunk in early:
+            a = axes[chunk][0]
+            wide = widen_half(chunk, side[a], teach_t)
+            teach_near.append(swap(wide, a))
 
         def g_rows(a, b):
             g_all = jnp.concatenate([g_own, near[a], g_core, swap(near[a], 'core')], axis=0)
             cols = g_all.T.reshape(2, 2, 2, dim // 8, g_all.shape[0])
-            cols = jnp.where(place['core'] == 0, cols[:, :, 0], cols[:, :, 1])
-            cols = jnp.where(place['x'] == 0, cols, cols[:, ::-1])
-            cols = jnp.where(place['y'] == 0, cols, cols[::-1])
+            cols = jnp.where(place_of['core'] == 0, cols[:, :, 0], cols[:, :, 1])
+            cols = jnp.where(place_of['x'] == 0, cols, cols[:, ::-1])
+            cols = jnp.where(place_of['y'] == 0, cols, cols[::-1])
             if b == 'x':
                 cols = jnp.swapaxes(cols, 0, 1)
             return cols[::-1].reshape(dim // 2, g_all.shape[0])
@@ -227,39 +350,40 @@
         rows_of = {'x': g_rows('x', 'y'), 'y': g_rows('y', 'x')}
 
         own_stats = local_stats(emb_loc, teach_t, g_t)
-        all_stats = lax.all_gather(own_stats[:4], 'tp')
-        sum_stu = jnp.sum(all_stats[:, 0], axis=0)
-        top = jnp.max(all_stats[:, 1], axis=0)
-        scale = jnp.exp(all_stats[:, 1] - top)
-        sum_tea = jnp.sum(all_stats[:, 2] * scale, axis=0)
-        cross = jnp.sum(all_stats[:, 3] * scale, axis=0)
+        all_stats = [own_stats] + [trade(own_stats, 'tp', k) for k in range(1, tp)]
+        sum_stu, top, sum_tea, cross = tree([tuple(st[i] for i in range(4)) for st in all_stats], join_stats)
         kl_tok = cross / sum_tea - (top + jnp.log(sum_tea)) + (SOFT_CAP + jnp.log(sum_stu))
-        loss_val = lax.psum(jnp.sum(weight * kl_tok), 'dp')
+        loss_part = jnp.sum(weight * kl_tok)
         stats = jnp.stack([weight / sum_stu, top, weight / sum_tea] + [jnp.zeros_like(top)] * 5)
+        stats_near = {axis: swap(stats, axis) for axis in 'xy'}
+        g_near_t = {axis: lax.optimization_barrier(near[axis]).T.astype(jnp.bfloat16) for axis in 'xy'}
 
         grad_part = jnp.zeros(hid_loc.shape, jnp.float32)
-        side = {axis: place[axis].astype(jnp.int32)[None] for axis in 'xy'}
-        grad_emb = jnp.zeros((dim // 8, vocab), jnp.float32)
+        pieces = {}
+        for chunk in late + early:
+            a = axes[chunk][0]
+            *send, own, grad_part = chunk_grad(chunk, chunk in late, side[a], emb_loc, teach_t, g_t, stats, grad_part)
+            if chunk in late:
+                got = swap(send[0], a)
+            else:
+                got = near_grad(chunk, side[a], emb_loc, teach_near[chunk], g_near_t[a], stats_near[a])
+            pieces[chunk] = (own, got, swap(own, 'core'), swap(got, 'core'))
+
+        grad_emb = None
         for chunk in range(CHUNKS):
-            a, b = ('x', 'y') if chunk % 2 == 0 else ('y', 'x')
-            send, own, grad_part = chunk_grad(chunk, side[a], emb_loc, teach_t, g_t, stats, grad_part)
-            got = swap(send, a)
-            pieces = (own, got, swap(own, 'core'), swap(got, 'core'))
-            send_b, keep, give = chunk_table(pieces, rows_of[a])
+            a, b = axes[chunk]
+            send_b, keep, give = chunk_table(pieces[chunk], rows_of[a])
             got_b = swap(send_b, b)
             mine = keep + got_b[: dim // 8]
-            other = swap(give + got_b[dim // 8 :], a)
-            low = jnp.where(place[a] == 0, mine, other)
-            high = jnp.where(place[a] == 0, other, mine)
-            start = chunk * 2 * HALF
-            grad_emb = lax.dynamic_update_slice(grad_emb, low, (0, start))
-            stop = min(vocab, start + 2 * HALF)
-            grad_emb = lax.dynamic_update_slice(grad_emb, high[:, : stop - start - HALF], (0, start + HALF))
-
-        grad_normed = lax.psum(grad_part, 'tp')
+            give = give + got_b[dim // 8 :]
+            other = swap(give, a)
+            grad_emb = place(chunk, side[a], mine, other, vocab, grad_emb)
+
+        grad_normed = grad_part
+        for k in range(tp.bit_length() - 1):
+            grad_normed = grad_normed + trade(grad_normed, 'tp', 1 << k)
         grad_hid, grad_scale = norm_pull(grad_normed)
-        grad_w = lax.psum(grad_scale, 'dp')
+        loss_val, grad_w = lax.psum((loss_part, grad_scale), 'dp')
         return loss_val, grad_hid.astype(jnp.bfloat16), grad_emb.T, grad_w
 
-
     return jax.shard_map(device_fn, mesh=mesh, in_specs=(P('dp', None), P(None), P('tp', None), P('dp', 'tp'), P('dp')), out_specs=(P(), P('dp', None), P('tp', 'dp'), P(None)), check_vma=False)

time: 719 us -> 858 us (1.19)
  waiting for transfers between devices: 273 us -> 363 us
  Pallas kernels: 271 us -> 325 us
  starting transfers between devices: 38 us -> 59.9 us
  local copies, waits for them, and re-layouts: 27.4 us -> 12.7 us
  between operations: 15.1 us -> 1.2 us
    ppermute x55 -> x69, waiting for transfers between devices: 247 us -> 363 us  [trade(): return lax.ppermute(a, axis, [(i, i ^ mask) for i in range(size)])]
    pallas_call x0 -> x18, Pallas kernels: none -> 55.1 us  [the longest x10 26.7 us: place(): pl.pallas_call(place_kernel, out_shape=jax.ShapeDtypeStruct((cols, vocab)...]
    psum x1 -> x0, waiting for transfers between devices: 26.1 us -> none  [device_fn(): grad_normed = lax.psum(grad_part, 'tp')]
    ppermute x55 -> x69, starting transfers between devices: 37.9 us -> 59.9 us  [trade(): return lax.ppermute(a, axis, [(i, i ^ mask) for i in range(size)])]
    dynamic_update_slice x19 -> x0, other arithmetic: 15.1 us -> none  [the longest x10 10.2 us: device_fn(): lax.dynamic_update_slice(grad_emb, high[:, :stop - start - HALF], (0, sta...]
    all_gather x1 -> x0, blocking collectives: 13.4 us -> none  [device_fn(): all_stats = lax.all_gather(own_stats[:4], 'tp')]
    psum x2 -> x1, blocking collectives: 27.9 us -> 41.1 us  [device_fn(): loss_val, grad_w = lax.psum((loss_part, grad_scale), 'dp')]
    unnamed x113 -> x78, local copies, waits for them, and re-layouts: 15.7 us -> 3.97 us
  transfers between devices with their start and end apart: 56 -> 69, of which waited for: 21 -> 21; matrix products, arithmetic and copies ran while one was open for 9% -> 6% of each run, Pallas kernels for 38% -> 38%
where the time goes in v2:
time: 858 us; the launch traced here: 847 us
  waiting for transfers between devices  363 us (42%)
  Pallas kernels  325 us (38%)
  starting transfers between devices  59.9 us (7%)
  other arithmetic  44.5 us (5%)
  blocking collectives  41.1 us (5%)
  local copies, waits for them, and re-layouts  12.7 us (1%)
    ppermute x69, waiting for transfers between devices, trade(): return lax.ppermute(a, axis, [(i, i ^ mask) for i in range(size)])  363 us
    pallas_call x10, Pallas kernels, chunk_grad(): pl.pallas_call(functools.partial(grad_kernel, limit, first, nb), out_shap...  138 us
    pallas_call x10, Pallas kernels, chunk_table(): pl.pallas_call(table_kernel, out_shape=(shape(2), shape(1), shape(1)), gr...  79.1 us
    ppermute x69, starting transfers between devices, trade(): return lax.ppermute(a, axis, [(i, i ^ mask) for i in range(size)])  59.9 us
    pallas_call x1, Pallas kernels, local_stats(): pl.pallas_call(functools.partial(stats_kernel, vocab), out_shape=jax.Shap...  52.2 us
    psum x1, blocking collectives, device_fn(): loss_val, grad_w = lax.psum((loss_part, grad_scale), 'dp')  41.1 us
    pallas_call x10, Pallas kernels, place(): pl.pallas_call(place_kernel, out_shape=jax.ShapeDtypeStruct((cols, vocab)...  26.7 us
    add x10, other arithmetic, device_fn(): give = give + got_b[dim // 8:]  19.5 us
  transfers between devices with their start and end apart: 69, of which 21 were waited for; matrix products, arithmetic and copies ran while one was open for 6% of the time, Pallas kernels for 38%

profile of v2, /device:TPU:0, one launch (start us, length us, event | category | flops | bytes accessed | tf_op | source)
XLA Modules:
  0.0 847.3 jit_solution(13823412502018172116)
XLA Ops:
  2.6 4.0 collective-permute-start.5
  14.1 52.2 %stats.1 = f32[8,256]{1,0:T(8,128)} custom-call(bf16[37984,896]{1,0:T(8,128)(2,1)} %e_ref.29, bf16[37984,256]{1,0:T(8,128)(2,1)} %bitcast.60, bf16[896,256]{1,0:T(8,128)(2,1)} %bitcast.76), custom_call_target="tpu_custom_call" | custom-call | flops 17425235968 | bytes 87515136 | tf_op jit(solution)/shard_map/stats/pallas_call | solution.py:72
  67.3 2.8 collective-permute-start.8
  82.4 13.8 %grad.10 = (f32[1920,256]{1,0:T(8,128)}, f32[1920,256]{1,0:T(8,128)}, f32[256,896]{1,0:T(8,128)}) custom-call(s32[1]{0:T(128)} %bitcast.20.side_ref, bf16[37984,896]{1,0:T(8,128)(2,1)} %e_ref.29, bf16[37984,256]{1,0:T(8,128)(2,1)} %bitcast.61, bf16[896,256]{1,0:T(8,128)(2,1)} %bitcast.77, f32[8,256]{1,0:T(8,128)} %stack.16.st_ref, ...), custom_call_target="tpu_custom_call" | custom-call | flops 3523215360 | bytes 12779520 | tf_op jit(solution)/shard_map/grad/pallas_call | solution.py:142
  96.2 13.9 %grad.11 = (f32[1920,256]{1,0:T(8,128)}, f32[1920,256]{1,0:T(8,128)}, f32[256,896]{1,0:T(8,128)}) custom-call(s32[1]{0:T(128)} %bitcast.16.side_ref, bf16[37984,896]{1,0:T(8,128)(2,1)} %e_ref.29, bf16[37984,256]{1,0:T(8,128)(2,1)} %bitcast.62, bf16[896,256]{1,0:T(8,128)(2,1)} %bitcast.78, f32[8,256]{1,0:T(8,128)} %stack.16.st_ref, ...), custom_call_target="tpu_custom_call" | custom-call | flops 3523215360 | bytes 12779520 | tf_op jit(solution)/shard_map/grad/pallas_call | solution.py:142
  110.1 13.8 %grad.12 = (f32[1920,256]{1,0:T(8,128)}, f32[1920,256]{1,0:T(8,128)}, f32[256,896]{1,0:T(8,128)}) custom-call(s32[1]{0:T(128)} %bitcast.20.side_ref, bf16[37984,896]{1,0:T(8,128)(2,1)} %e_ref.29, bf16[37984,256]{1,0:T(8,128)(2,1)} %bitcast.63, bf16[896,256]{1,0:T(8,128)(2,1)} %bitcast.79, f32[8,256]{1,0:T(8,128)} %stack.16.st_ref, ...), custom_call_target="tpu_custom_call" | custom-call | flops 3523215360 | bytes 12779520 | tf_op jit(solution)/shard_map/grad/pallas_call | solution.py:142
  123.9 13.9 %grad.13 = (f32[1920,256]{1,0:T(8,128)}, f32[1920,256]{1,0:T(8,128)}, f32[256,896]{1,0:T(8,128)}) custom-call(s32[1]{0:T(128)} %bitcast.16.side_ref, bf16[37984,896]{1,0:T(8,128)(2,1)} %e_ref.29, bf16[37984,256]{1,0:T(8,128)(2,1)} %bitcast.64, bf16[896,256]{1,0:T(8,128)(2,1)} %bitcast.80, f32[8,256]{1,0:T(8,128)} %stack.16.st_ref, ...), custom_call_target="tpu_custom_call" | custom-call | flops 3523215360 | bytes 12779520 | tf_op jit(solution)/shard_map/grad/pallas_call | solution.py:142
  137.8 14.0 %grad.14 = (f32[1920,256]{1,0:T(8,128)}, f32[1920,256]{1,0:T(8,128)}, f32[256,896]{1,0:T(8,128)}) custom-call(s32[1]{0:T(128)} %bitcast.20.side_ref, bf16[37984,896]{1,0:T(8,128)(2,1)} %e_ref.29, bf16[37984,256]{1,0:T(8,128)(2,1)} %bitcast.65, bf16[896,256]{1,0:T(8,128)(2,1)} %bitcast.81, f32[8,256]{1,0:T(8,128)} %stack.16.st_ref, ...), custom_call_target="tpu_custom_call" | custom-call | flops 3523215360 | bytes 12779520 | tf_op jit(solution)/shard_map/grad/pallas_call | solution.py:142
  151.8 14.1 %grad.15 = (f32[1920,256]{1,0:T(8,128)}, f32[1920,256]{1,0:T(8,128)}, f32[256,896]{1,0:T(8,128)}) custom-call(s32[1]{0:T(128)} %bitcast.16.side_ref, bf16[37984,896]{1,0:T(8,128)(2,1)} %e_ref.29, bf16[37984,256]{1,0:T(8,128)(2,1)} %bitcast.66, bf16[896,256]{1,0:T(8,128)(2,1)} %bitcast.82, f32[8,256]{1,0:T(8,128)} %stack.16.st_ref, ...), custom_call_target="tpu_custom_call" | custom-call | flops 3523215360 | bytes 12779520 | tf_op jit(solution)/shard_map/grad/pallas_call | solution.py:142
  165.9 13.6 %grad.16 = (f32[1920,256]{1,0:T(8,128)}, f32[256,896]{1,0:T(8,128)}) custom-call(s32[1]{0:T(128)} %bitcast.20.side_ref, bf16[37984,896]{1,0:T(8,128)(2,1)} %e_ref.29, bf16[37984,256]{1,0:T(8,128)(2,1)} %bitcast.67, bf16[896,256]{1,0:T(8,128)(2,1)} %bitcast.83, f32[8,256]{1,0:T(8,128)} %stack.16.st_ref, f32[256,896]{1,0:T(8,128)} %get-tuple-element.65.acc_ref), custom_call_target="tpu_custom_call" | custom-call | flops 3523215360 | bytes 12779520 | tf_op jit(solution)/shard_map/grad/pallas_call | solution.py:142
  179.5 13.7 %grad.17 = (f32[1920,256]{1,0:T(8,128)}, f32[256,896]{1,0:T(8,128)}) custom-call(s32[1]{0:T(128)} %bitcast.16.side_ref, bf16[37984,896]{1,0:T(8,128)(2,1)} %e_ref.29, bf16[37984,256]{1,0:T(8,128)(2,1)} %bitcast.68, bf16[896,256]{1,0:T(8,128)(2,1)} %bitcast.84, f32[8,256]{1,0:T(8,128)} %stack.16.st_ref, f32[256,896]{1,0:T(8,128)} %get-tuple-element.66.acc_ref), custom_call_target="tpu_custom_call" | custom-call | flops 3523215360 | bytes 12779520 | tf_op jit(solution)/shard_map/grad/pallas_call | solution.py:142
  193.2 13.6 %grad.18 = (f32[1920,256]{1,0:T(8,128)}, f32[256,896]{1,0:T(8,128)}) custom-call(s32[1]{0:T(128)} %bitcast.20.side_ref, bf16[37984,896]{1,0:T(8,128)(2,1)} %e_ref.29, bf16[37984,256]{1,0:T(8,128)(2,1)} %bitcast.69, bf16[896,256]{1,0:T(8,128)(2,1)} %bitcast.85, f32[8,256]{1,0:T(8,128)} %stack.16.st_ref, f32[256,896]{1,0:T(8,128)} %get-tuple-element.67.acc_ref), custom_call_target="tpu_custom_call" | custom-call | flops 3523215360 | bytes 12779520 | tf_op jit(solution)/shard_map/grad/pallas_call | solution.py:142
  206.8 14.1 %grad.19 = (f32[1920,256]{1,0:T(8,128)}, f32[256,896]{1,0:T(8,128)}) custom-call(s32[1]{0:T(128)} %bitcast.16.side_ref, bf16[37984,896]{1,0:T(8,128)(2,1)} %e_ref.29, bf16[37984,256]{1,0:T(8,128)(2,1)} %bitcast.70, bf16[896,256]{1,0:T(8,128)(2,1)} %bitcast.86, f32[8,256]{1,0:T(8,128)} %stack.16.st_ref, f32[256,896]{1,0:T(8,128)} %get-tuple-element.68.acc_ref), custom_call_target="tpu_custom_call" | custom-call | flops 3523215360 | bytes 12779520 | tf_op jit(solution)/shard_map/grad/pallas_call | solution.py:142
  227.9 2.4 widen.4
  231.7 2.4 widen.5
  238.5 5.3 collective-permute-done.10
  244.9 2.4 widen.7
  249.3 27.1 %collective-permute-done.47.t_ref = f32[1920,256]{1,0:T(8,128)} collective-permute-done((f32[1920,256]{1,0:T(8,128)}, f32[1920,256]{1,0:T(8,128)}, u32[]{:S(2)}, u32[]{:S(2)}) %collective-permute-start.47) | collective-permute-done | bytes 1966112 | tf_op jit(solution)/shard_map/ppermute | solution.py:293
  276.4 3.7 collective-permute-done.53.t_ref
  280.9 37.7 %collective-permute-done.59.t_ref = f32[1920,256]{1,0:T(8,128)} collective-permute-done((f32[1920,256]{1,0:T(8,128)}, f32[1920,256]{1,0:T(8,128)}, u32[]{:S(2)}, u32[]{:S(2)}) %collective-permute-start.59) | collective-permute-done | bytes 1966112 | tf_op jit(solution)/shard_map/ppermute | solution.py:293
  318.5 3.7 collective-permute-done.64.t_ref
  323.7 40.6 %collective-permute-done.42.near_ref = f32[1920,256]{1,0:T(8,128)} collective-permute-done((f32[1920,256]{1,0:T(8,128)}, f32[1920,256]{1,0:T(8,128)}, u32[]{:S(2)}, u32[]{:S(2)}) %collective-permute-start.42) | collective-permute-done | bytes 1966112 | tf_op jit(solution)/shard_map/ppermute | solution.py:293
  366.8 39.7 %collective-permute-done.32.near_ref = f32[1920,256]{1,0:T(8,128)} collective-permute-done((f32[1920,256]{1,0:T(8,128)}, f32[1920,256]{1,0:T(8,128)}, u32[]{:S(2)}, u32[]{:S(2)}) %collective-permute-start.32) | collective-permute-done | bytes 1966112 | tf_op jit(solution)/shard_map/ppermute | solution.py:293
  407.0 2.9 collective-permute-done.27.near_ref
  410.5 33.8 %collective-permute-done.20.near_ref = f32[1920,256]{1,0:T(8,128)} collective-permute-done((f32[1920,256]{1,0:T(8,128)}, f32[1920,256]{1,0:T(8,128)}, u32[]{:S(2)}, u32[]{:S(2)}) %collective-permute-start.20) | collective-permute-done | bytes 1966112 | tf_op jit(solution)/shard_map/ppermute | solution.py:293
  447.0 4.7 near.4.near_ref
  454.0 4.7 near.5.near_ref
  459.0 4.7 near.6.near_ref
  463.9 4.7 near.7.near_ref
  469.0 22.8 %collective-permute-done.12.near_ref = f32[1920,256]{1,0:T(8,128)} collective-permute-done((f32[1920,256]{1,0:T(8,128)}, f32[1920,256]{1,0:T(8,128)}, u32[]{:S(2)}, u32[]{:S(2)}) %collective-permute-start.12) | collective-permute-done | bytes 1966112 | tf_op jit(solution)/shard_map/ppermute | solution.py:293
  493.7 2.8 fusion.1
  506.4 8.0 table.16
  515.5 2.4 reverse_select_fusion
  519.2 7.9 table.18
  527.1 7.9 table.17
  536.4 7.9 table.19
  544.3 7.9 table.15
  552.2 7.9 table.14
  560.8 7.9 table.13
  568.6 7.9 table.12
  576.5 8.0 table.11
  586.6 7.8 table.10
  596.0 2.9 slice_add_fusion.6
  602.5 2.7 slice_add_fusion.2
  605.2 20.1 %collective-permute-done.67 = f32[224,1920]{1,0:T(8,128)} collective-permute-done((f32[224,1920]{1,0:T(8,128)}, f32[224,1920]{1,0:T(8,128)}, u32[]{:S(2)}, u32[]{:S(2)}) %collective-permute-start.67) | collective-permute-done | bytes 1720352 | tf_op jit(solution)/shard_map/ppermute | solution.py:293
  626.6 2.7 slice_add_fusion
  629.2 32.9 %collective-permute-done.45 = f32[224,1920]{1,0:T(8,128)} collective-permute-done((f32[224,1920]{1,0:T(8,128)}, f32[224,1920]{1,0:T(8,128)}, u32[]{:S(2)}, u32[]{:S(2)}) %collective-permute-start.45) | collective-permute-done | bytes 1720352 | tf_op jit(solution)/shard_map/ppermute | solution.py:293
  663.7 2.6 slice_add_fusion.8
  666.3 2.9 collective-permute-start.11
  670.7 28.2 %collective-permute-done.35 = f32[224,1920]{1,0:T(8,128)S(1)} collective-permute-done((f32[224,1920]{1,0:T(8,128)S(1)}, f32[224,1920]{1,0:T(8,128)S(1)}, u32[]{:S(2)}, u32[]{:S(2)}) %collective-permute-start.35) | collective-permute-done | bytes 1720352 | tf_op jit(solution)/shard_map/ppermute | solution.py:293
  707.8 28.0 %collective-permute-done.25 = f32[224,1920]{1,0:T(8,128)S(1)} collective-permute-done((f32[224,1920]{1,0:T(8,128)S(1)}, f32[224,1920]{1,0:T(8,128)S(1)}, u32[]{:S(2)}, u32[]{:S(2)}) %collective-permute-start.25) | collective-permute-done | bytes 1720352 | tf_op jit(solution)/shard_map/ppermute | solution.py:293
  741.3 13.0 %collective-permute-done.52.other_ref = f32[112,1920]{1,0:T(8,128)} collective-permute-done((f32[112,1920]{1,0:T(8,128)S(1)}, f32[112,1920]{1,0:T(8,128)}, u32[]{:S(2)}, u32[]{:S(2)}) %collective-permute-start.52) | collective-permute-done | bytes 860192 | tf_op jit(solution)/shard_map/ppermute | solution.py:293
  756.6 16.2 %collective-permute-done.63.other_ref = f32[112,1920]{1,0:T(8,128)} collective-permute-done((f32[112,1920]{1,0:T(8,128)S(1)}, f32[112,1920]{1,0:T(8,128)}, u32[]{:S(2)}, u32[]{:S(2)}) %collective-permute-start.63) | collective-permute-done | bytes 860192 | tf_op jit(solution)/shard_map/ppermute | solution.py:293
  778.1 41.1 %all-reduce = (f32[]{:T(128)}, f32[896]{0:T(1024)}) all-reduce(f32[]{:T(128)} %get-tuple-element.164, f32[896]{0:T(1024)S(1)} %get-tuple-element.120), channel_id=1, replica_groups=mesh['tp'=4,'dp'=8] {'dp'}, use_global_device_ids=true, to_apply=%region_3.4 | all-reduce | flops 897 | bytes 7176 | tf_op jit(solution)/shard_map/psum | solution.py:386
  820.4 2.7 place.10.refs_0_
  823.1 2.7 place.11.refs_0_
  825.8 2.7 place.12.refs_0_
  828.5 2.7 place.13.refs_0_
  831.1 2.7 place.14.refs_0_
  833.8 2.7 place.15.refs_0_
  836.5 2.7 place.16.refs_0_
  839.2 2.7 place.17.refs_0_
  841.9 2.7 place.18.refs_0_
  844.5 2.6 place.19
  (236 shorter events, 101.0 us)
Async XLA Ops:
  2.6 11.1 %collective-permute-start.5 = (f32[8,128]{1,0:T(8,128)S(1)}, f32[8,128]{1,0:T(8,128)S(1)}, u32[]{:S(2)}, u32[]{:S(2)}) collective-permute-start(f32[8,128]{1,0:T(8,128)S(1)} %broadcast_in_dim.17), channel_id=1, source_target_pairs={{0,6},{1,7},{2,4},{3,5},{4,2},{5,3},{6,0},{7,1},{8,14},{9,15},{10,... | collective-permute-start | bytes 12296 | tf_op jit(solution)/shard_map/ppermute | solution.py:293
  6.6 60.7 %collective-permute-start.3 = (f32[8,128]{1,0:T(8,128)S(1)}, f32[8,128]{1,0:T(8,128)S(1)}, u32[]{:S(2)}, u32[]{:S(2)}) collective-permute-start(f32[8,128]{1,0:T(8,128)S(1)} %broadcast_in_dim.17), channel_id=1, source_target_pairs={{0,4},{1,5},{2,6},{3,7},{4,0},{5,1},{6,2},{7,3},{8,12},{9,13},{10,... | collective-permute-start | bytes 12296 | tf_op jit(solution)/shard_map/ppermute | solution.py:293
  7.7 62.3 %collective-permute-start.2 = (f32[8,128]{1,0:T(8,128)S(1)}, f32[8,128]{1,0:T(8,128)S(1)}, u32[]{:S(2)}, u32[]{:S(2)}) collective-permute-start(f32[8,128]{1,0:T(8,128)S(1)} %broadcast_in_dim.17), channel_id=1, source_target_pairs={{0,3},{1,2},{2,1},{3,0},{4,7},{5,6},{6,5},{7,4},{8,11},{9,10},{10,... | collective-permute-start | bytes 12296 | tf_op jit(solution)/shard_map/ppermute | solution.py:293
  8.6 63.1 %collective-permute-start.1 = (f32[8,128]{1,0:T(8,128)S(1)}, f32[8,128]{1,0:T(8,128)S(1)}, u32[]{:S(2)}, u32[]{:S(2)}) collective-permute-start(f32[8,128]{1,0:T(8,128)S(1)} %broadcast_in_dim.17), channel_id=1, source_target_pairs={{0,2},{1,3},{2,0},{3,1},{4,6},{5,7},{6,4},{7,5},{8,10},{9,11},{10,... | collective-permute-start | bytes 12296 | tf_op jit(solution)/shard_map/ppermute | solution.py:293
  13.7 58.0 %collective-permute-start.6 = (f32[8,128]{1,0:T(8,128)S(1)}, f32[8,128]{1,0:T(8,128)S(1)}, u32[]{:S(2)}, u32[]{:S(2)}) collective-permute-start(f32[8,128]{1,0:T(8,128)S(1)} %broadcast_in_dim.17), channel_id=1, source_target_pairs={{0,7},{1,6},{2,5},{3,4},{4,3},{5,2},{6,1},{7,0},{8,15},{9,14},{10,... | collective-permute-start | bytes 12296 | tf_op jit(solution)/shard_map/ppermute | solution.py:293
  13.7 59.7 %collective-permute-start = (f32[8,128]{1,0:T(8,128)S(1)}, f32[8,128]{1,0:T(8,128)S(1)}, u32[]{:S(2)}, u32[]{:S(2)}) collective-permute-start(f32[8,128]{1,0:T(8,128)S(1)} %broadcast_in_dim.17), channel_id=1, source_target_pairs={{0,1},{1,0},{2,3},{3,2},{4,5},{5,4},{6,7},{7,6},{8,9},{9,8},{10,11... | collective-permute-start | bytes 12296 | tf_op jit(solution)/shard_map/ppermute | solution.py:293
  67.3 7.3 collective-permute-start.8
  71.7 162.4 %collective-permute-start.23 = (f32[256,896]{0,1:T(8,128)}, f32[256,896]{0,1:T(8,128)}, u32[]{:S(2)}, u32[]{:S(2)}) collective-permute-start(f32[256,896]{0,1:T(8,128)} %convert_element_type.33), channel_id=1, source_target_pairs={{0,2},{1,3},{2,0},{3,1},{4,6},{5,7},{6,4},{7,5},{8,10},{9,11},{10,... | collective-permute-start | bytes 2752520 | tf_op jit(solution)/shard_map/ppermute | solution.py:293
  73.4 162.2 %collective-permute-start.16 = (f32[256,896]{0,1:T(8,128)}, f32[256,896]{0,1:T(8,128)}, u32[]{:S(2)}, u32[]{:S(2)}) collective-permute-start(f32[256,896]{0,1:T(8,128)} %convert_element_type.33), channel_id=1, source_target_pairs={{0,1},{1,0},{2,3},{3,2},{4,5},{5,4},{6,7},{7,6},{8,9},{9,8},{10,11... | collective-permute-start | bytes 2752520 | tf_op jit(solution)/shard_map/ppermute | solution.py:293
  74.6 161.0 %collective-permute-start.15 = (f32[256,896]{0,1:T(8,128)}, f32[256,896]{0,1:T(8,128)}, u32[]{:S(2)}, u32[]{:S(2)}) collective-permute-start(f32[256,896]{0,1:T(8,128)} %convert_element_type.33), channel_id=1, source_target_pairs={{0,4},{1,5},{2,6},{3,7},{4,0},{5,1},{6,2},{7,3},{8,12},{9,13},{10,... | collective-permute-start | bytes 2752520 | tf_op jit(solution)/shard_map/ppermute | solution.py:293
  222.4 21.4 %collective-permute-start.10 = (f32[256,896]{0,1:T(8,128)S(1)}, f32[256,896]{0,1:T(8,128)}, u32[]{:S(2)}, u32[]{:S(2)}) collective-permute-start(f32[256,896]{0,1:T(8,128)S(1)} %copy.20), channel_id=1, source_target_pairs={{0,8},{8,0},{16,24},{24,16},{1,9},{9,1},{17,25},{25,17},{2,10},{10... | collective-permute-start | bytes 2752520 | tf_op jit(solution)/shard_map/ppermute | solution.py:293
  230.3 46.1 %collective-permute-start.47 = (f32[1920,256]{1,0:T(8,128)}, f32[1920,256]{1,0:T(8,128)}, u32[]{:S(2)}, u32[]{:S(2)}) collective-permute-start(f32[1920,256]{1,0:T(8,128)} %widen.4), channel_id=1, source_target_pairs={{0,4},{1,5},{2,6},{3,7},{4,0},{5,1},{6,2},{7,3},{8,12},{9,13},{10,... | collective-permute-start | bytes 5898248 | tf_op jit(solution)/shard_map/ppermute | solution.py:293
  234.1 46.0 %collective-permute-start.53 = (f32[1920,256]{1,0:T(8,128)}, f32[1920,256]{1,0:T(8,128)}, u32[]{:S(2)}, u32[]{:S(2)}) collective-permute-start(f32[1920,256]{1,0:T(8,128)} %widen.5), channel_id=1, source_target_pairs={{0,2},{1,3},{2,0},{3,1},{4,6},{5,7},{6,4},{7,5},{8,10},{9,11},{10,... | collective-permute-start | bytes 5898248 | tf_op jit(solution)/shard_map/ppermute | solution.py:293
  235.6 11.7 %collective-permute-start.24 = (f32[256,896]{0,1:T(8,128)}, f32[256,896]{0,1:T(8,128)S(1)}, u32[]{:S(2)}, u32[]{:S(2)}) collective-permute-start(f32[256,896]{0,1:T(8,128)} %collective-permute-done.23), channel_id=1, source_target_pairs={{0,1},{1,0},{2,3},{3,2},{4,5},{5,4},{6,7},{7,6},{8,9},{9,8},{10,11... | collective-permute-start | bytes 2752520 | tf_op jit(solution)/shard_map/ppermute | solution.py:293
  235.6 13.1 %collective-permute-start.17 = (f32[256,896]{0,1:T(8,128)}, f32[256,896]{0,1:T(8,128)S(1)}, u32[]{:S(2)}, u32[]{:S(2)}) collective-permute-start(f32[256,896]{0,1:T(8,128)} %collective-permute-done.15), channel_id=1, source_target_pairs={{0,1},{1,0},{2,3},{3,2},{4,5},{5,4},{6,7},{7,6},{8,9},{9,8},{10,11... | collective-permute-start | bytes 2752520 | tf_op jit(solution)/shard_map/ppermute | solution.py:293
  243.8 74.7 %collective-permute-start.59 = (f32[1920,256]{1,0:T(8,128)}, f32[1920,256]{1,0:T(8,128)}, u32[]{:S(2)}, u32[]{:S(2)}) collective-permute-start(f32[1920,256]{1,0:T(8,128)} %widen.6), channel_id=1, source_target_pairs={{0,4},{1,5},{2,6},{3,7},{4,0},{5,1},{6,2},{7,3},{8,12},{9,13},{10,... | collective-permute-start | bytes 5898248 | tf_op jit(solution)/shard_map/ppermute | solution.py:293
  247.3 75.0 %collective-permute-start.64 = (f32[1920,256]{1,0:T(8,128)}, f32[1920,256]{1,0:T(8,128)}, u32[]{:S(2)}, u32[]{:S(2)}) collective-permute-start(f32[1920,256]{1,0:T(8,128)} %widen.7), channel_id=1, source_target_pairs={{0,2},{1,3},{2,0},{3,1},{4,6},{5,7},{6,4},{7,5},{8,10},{9,11},{10,... | collective-permute-start | bytes 5898248 | tf_op jit(solution)/shard_map/ppermute | solution.py:293
  248.8 115.6 %collective-permute-start.42 = (f32[1920,256]{1,0:T(8,128)}, f32[1920,256]{1,0:T(8,128)}, u32[]{:S(2)}, u32[]{:S(2)}) collective-permute-start(f32[1920,256]{1,0:T(8,128)} %get-tuple-element.96), channel_id=1, source_target_pairs={{0,2},{1,3},{2,0},{3,1},{4,6},{5,7},{6,4},{7,5},{8,10},{9,11},{10,... | collective-permute-start | bytes 5898248 | tf_op jit(solution)/shard_map/ppermute | solution.py:293
  276.4 88.0 %collective-permute-start.43 = (f32[1920,256]{1,0:T(8,128)}, f32[1920,256]{1,0:T(8,128)}, u32[]{:S(2)}, u32[]{:S(2)}) collective-permute-start(f32[1920,256]{1,0:T(8,128)} %get-tuple-element.95.own_ref), channel_id=1, source_target_pairs={{0,1},{1,0},{2,3},{3,2},{4,5},{5,4},{6,7},{7,6},{8,9},{9,8},{10,11... | collective-permute-start | bytes 5898248 | tf_op jit(solution)/shard_map/ppermute | solution.py:293
  280.1 85.0 %collective-permute-start.37 = (f32[1920,256]{1,0:T(8,128)}, f32[1920,256]{1,0:T(8,128)}, u32[]{:S(2)}, u32[]{:S(2)}) collective-permute-start(f32[1920,256]{1,0:T(8,128)} %get-tuple-element.91), channel_id=1, source_target_pairs={{0,4},{1,5},{2,6},{3,7},{4,0},{5,1},{6,2},{7,3},{8,12},{9,13},{10,... | collective-permute-start | bytes 5898248 | tf_op jit(solution)/shard_map/ppermute | solution.py:293
  318.5 46.8 %collective-permute-start.38 = (f32[1920,256]{1,0:T(8,128)}, f32[1920,256]{1,0:T(8,128)}, u32[]{:S(2)}, u32[]{:S(2)}) collective-permute-start(f32[1920,256]{1,0:T(8,128)} %get-tuple-element.90.own_ref), channel_id=1, source_target_pairs={{0,1},{1,0},{2,3},{3,2},{4,5},{5,4},{6,7},{7,6},{8,9},{9,8},{10,11... | collective-permute-start | bytes 5898248 | tf_op jit(solution)/shard_map/ppermute | solution.py:293
  322.3 84.3 %collective-permute-start.32 = (f32[1920,256]{1,0:T(8,128)}, f32[1920,256]{1,0:T(8,128)}, u32[]{:S(2)}, u32[]{:S(2)}) collective-permute-start(f32[1920,256]{1,0:T(8,128)} %get-tuple-element.86), channel_id=1, source_target_pairs={{0,2},{1,3},{2,0},{3,1},{4,6},{5,7},{6,4},{7,5},{8,10},{9,11},{10,... | collective-permute-start | bytes 5898248 | tf_op jit(solution)/shard_map/ppermute | solution.py:293
  364.4 42.1 %collective-permute-start.33 = (f32[1920,256]{1,0:T(8,128)}, f32[1920,256]{1,0:T(8,128)}, u32[]{:S(2)}, u32[]{:S(2)}) collective-permute-start(f32[1920,256]{1,0:T(8,128)} %get-tuple-element.85.own_ref), channel_id=1, source_target_pairs={{0,1},{1,0},{2,3},{3,2},{4,5},{5,4},{6,7},{7,6},{8,9},{9,8},{10,11... | collective-permute-start | bytes 5898248 | tf_op jit(solution)/shard_map/ppermute | solution.py:293
  364.4 45.5 %collective-permute-start.27 = (f32[1920,256]{1,0:T(8,128)}, f32[1920,256]{1,0:T(8,128)}, u32[]{:S(2)}, u32[]{:S(2)}) collective-permute-start(f32[1920,256]{1,0:T(8,128)} %get-tuple-element.81), channel_id=1, source_target_pairs={{0,4},{1,5},{2,6},{3,7},{4,0},{5,1},{6,2},{7,3},{8,12},{9,13},{10,... | collective-permute-start | bytes 5898248 | tf_op jit(solution)/shard_map/ppermute | solution.py:293
  365.1 44.8 %collective-permute-start.28 = (f32[1920,256]{1,0:T(8,128)}, f32[1920,256]{1,0:T(8,128)}, u32[]{:S(2)}, u32[]{:S(2)}) collective-permute-start(f32[1920,256]{1,0:T(8,128)} %get-tuple-element.80.own_ref), channel_id=1, source_target_pairs={{0,1},{1,0},{2,3},{3,2},{4,5},{5,4},{6,7},{7,6},{8,9},{9,8},{10,11... | collective-permute-start | bytes 5898248 | tf_op jit(solution)/shard_map/ppermute | solution.py:293
  365.4 78.9 %collective-permute-start.20 = (f32[1920,256]{1,0:T(8,128)}, f32[1920,256]{1,0:T(8,128)}, u32[]{:S(2)}, u32[]{:S(2)}) collective-permute-start(f32[1920,256]{1,0:T(8,128)} %get-tuple-element.76), channel_id=1, source_target_pairs={{0,2},{1,3},{2,0},{3,1},{4,6},{5,7},{6,4},{7,5},{8,10},{9,11},{10,... | collective-permute-start | bytes 5898248 | tf_op jit(solution)/shard_map/ppermute | solution.py:293
  406.5 39.7 %collective-permute-start.21 = (f32[1920,256]{1,0:T(8,128)}, f32[1920,256]{1,0:T(8,128)}, u32[]{:S(2)}, u32[]{:S(2)}) collective-permute-start(f32[1920,256]{1,0:T(8,128)} %get-tuple-element.75.own_ref), channel_id=1, source_target_pairs={{0,1},{1,0},{2,3},{3,2},{4,5},{5,4},{6,7},{7,6},{8,9},{9,8},{10,11... | collective-permute-start | bytes 5898248 | tf_op jit(solution)/shard_map/ppermute | solution.py:293
  406.5 45.2 %collective-permute-start.49 = (f32[1920,256]{1,0:T(8,128)}, f32[1920,256]{1,0:T(8,128)}, u32[]{:S(2)}, u32[]{:S(2)}) collective-permute-start(f32[1920,256]{1,0:T(8,128)} %get-tuple-element.100.own_ref), channel_id=1, source_target_pairs={{0,1},{1,0},{2,3},{3,2},{4,5},{5,4},{6,7},{7,6},{8,9},{9,8},{10,11... | collective-permute-start | bytes 5898248 | tf_op jit(solution)/shard_map/ppermute | solution.py:293
  409.9 48.8 %collective-permute-start.55 = (f32[1920,256]{1,0:T(8,128)}, f32[1920,256]{1,0:T(8,128)}, u32[]{:S(2)}, u32[]{:S(2)}) collective-permute-start(f32[1920,256]{1,0:T(8,128)} %get-tuple-element.104.own_ref), channel_id=1, source_target_pairs={{0,1},{1,0},{2,3},{3,2},{4,5},{5,4},{6,7},{7,6},{8,9},{9,8},{10,11... | collective-permute-start | bytes 5898248 | tf_op jit(solution)/shard_map/ppermute | solution.py:293
  409.9 53.8 %collective-permute-start.60 = (f32[1920,256]{1,0:T(8,128)}, f32[1920,256]{1,0:T(8,128)}, u32[]{:S(2)}, u32[]{:S(2)}) collective-permute-start(f32[1920,256]{1,0:T(8,128)} %get-tuple-element.108.own_ref), channel_id=1, source_target_pairs={{0,1},{1,0},{2,3},{3,2},{4,5},{5,4},{6,7},{7,6},{8,9},{9,8},{10,11... | collective-permute-start | bytes 5898248 | tf_op jit(solution)/shard_map/ppermute | solution.py:293
  444.2 24.4 %collective-permute-start.65 = (f32[1920,256]{1,0:T(8,128)}, f32[1920,256]{1,0:T(8,128)}, u32[]{:S(2)}, u32[]{:S(2)}) collective-permute-start(f32[1920,256]{1,0:T(8,128)} %get-tuple-element.112.own_ref), channel_id=1, source_target_pairs={{0,1},{1,0},{2,3},{3,2},{4,5},{5,4},{6,7},{7,6},{8,9},{9,8},{10,11... | collective-permute-start | bytes 5898248 | tf_op jit(solution)/shard_map/ppermute | solution.py:293
  446.2 45.5 %collective-permute-start.12 = (f32[1920,256]{1,0:T(8,128)}, f32[1920,256]{1,0:T(8,128)}, u32[]{:S(2)}, u32[]{:S(2)}) collective-permute-start(f32[1920,256]{1,0:T(8,128)} %get-tuple-element.71), channel_id=1, source_target_pairs={{0,4},{1,5},{2,6},{3,7},{4,0},{5,1},{6,2},{7,3},{8,12},{9,13},{10,... | collective-permute-start | bytes 5898248 | tf_op jit(solution)/shard_map/ppermute | solution.py:293
  451.7 40.1 %collective-permute-start.50 = (f32[1920,256]{1,0:T(8,128)}, f32[1920,256]{1,0:T(8,128)}, u32[]{:S(2)}, u32[]{:S(2)}) collective-permute-start(f32[1920,256]{1,0:T(8,128)} %near.4.near_ref), channel_id=1, source_target_pairs={{0,1},{1,0},{2,3},{3,2},{4,5},{5,4},{6,7},{7,6},{8,9},{9,8},{10,11... | collective-permute-start | bytes 5898248 | tf_op jit(solution)/shard_map/ppermute | solution.py:293
  458.7 33.6 %collective-permute-start.56 = (f32[1920,256]{1,0:T(8,128)}, f32[1920,256]{1,0:T(8,128)}, u32[]{:S(2)}, u32[]{:S(2)}) collective-permute-start(f32[1920,256]{1,0:T(8,128)} %near.5.near_ref), channel_id=1, source_target_pairs={{0,1},{1,0},{2,3},{3,2},{4,5},{5,4},{6,7},{7,6},{8,9},{9,8},{10,11... | collective-permute-start | bytes 5898248 | tf_op jit(solution)/shard_map/ppermute | solution.py:293
  463.7 32.7 %collective-permute-start.61 = (f32[1920,256]{1,0:T(8,128)}, f32[1920,256]{1,0:T(8,128)}, u32[]{:S(2)}, u32[]{:S(2)}) collective-permute-start(f32[1920,256]{1,0:T(8,128)} %near.6.near_ref), channel_id=1, source_target_pairs={{0,1},{1,0},{2,3},{3,2},{4,5},{5,4},{6,7},{7,6},{8,9},{9,8},{10,11... | collective-permute-start | bytes 5898248 | tf_op jit(solution)/shard_map/ppermute | solution.py:293
  468.7 30.5 %collective-permute-start.66 = (f32[1920,256]{1,0:T(8,128)}, f32[1920,256]{1,0:T(8,128)}, u32[]{:S(2)}, u32[]{:S(2)}) collective-permute-start(f32[1920,256]{1,0:T(8,128)} %near.7.near_ref), channel_id=1, source_target_pairs={{0,1},{1,0},{2,3},{3,2},{4,5},{5,4},{6,7},{7,6},{8,9},{9,8},{10,11... | collective-permute-start | bytes 5898248 | tf_op jit(solution)/shard_map/ppermute | solution.py:293
  491.8 12.5 %collective-permute-start.44 = (f32[1920,256]{1,0:T(8,128)}, f32[1920,256]{1,0:T(8,128)}, u32[]{:S(2)}, u32[]{:S(2)}) collective-permute-start(f32[1920,256]{1,0:T(8,128)} %collective-permute-done.42.near_ref), channel_id=1, source_target_pairs={{0,1},{1,0},{2,3},{3,2},{4,5},{5,4},{6,7},{7,6},{8,9},{9,8},{10,11... | collective-permute-start | bytes 5898248 | tf_op jit(solution)/shard_map/ppermute | solution.py:293
  491.8 12.9 %collective-permute-start.39 = (f32[1920,256]{1,0:T(8,128)}, f32[1920,256]{1,0:T(8,128)}, u32[]{:S(2)}, u32[]{:S(2)}) collective-permute-start(f32[1920,256]{1,0:T(8,128)} %collective-permute-done.37.near_ref), channel_id=1, source_target_pairs={{0,1},{1,0},{2,3},{3,2},{4,5},{5,4},{6,7},{7,6},{8,9},{9,8},{10,11... | collective-permute-start | bytes 5898248 | tf_op jit(solution)/shard_map/ppermute | solution.py:293
  492.3 22.1 %collective-permute-start.34 = (f32[1920,256]{1,0:T(8,128)}, f32[1920,256]{1,0:T(8,128)}, u32[]{:S(2)}, u32[]{:S(2)}) collective-permute-start(f32[1920,256]{1,0:T(8,128)} %collective-permute-done.32.near_ref), channel_id=1, source_target_pairs={{0,1},{1,0},{2,3},{3,2},{4,5},{5,4},{6,7},{7,6},{8,9},{9,8},{10,11... | collective-permute-start | bytes 5898248 | tf_op jit(solution)/shard_map/ppermute | solution.py:293
  496.4 38.6 %collective-permute-start.29 = (f32[1920,256]{1,0:T(8,128)}, f32[1920,256]{1,0:T(8,128)}, u32[]{:S(2)}, u32[]{:S(2)}) collective-permute-start(f32[1920,256]{1,0:T(8,128)} %collective-permute-done.27.near_ref), channel_id=1, source_target_pairs={{0,1},{1,0},{2,3},{3,2},{4,5},{5,4},{6,7},{7,6},{8,9},{9,8},{10,11... | collective-permute-start | bytes 5898248 | tf_op jit(solution)/shard_map/ppermute | solution.py:293
  499.2 60.9 %collective-permute-start.22 = (f32[1920,256]{1,0:T(8,128)}, f32[1920,256]{1,0:T(8,128)}, u32[]{:S(2)}, u32[]{:S(2)}) collective-permute-start(f32[1920,256]{1,0:T(8,128)} %collective-permute-done.20.near_ref), channel_id=1, source_target_pairs={{0,1},{1,0},{2,3},{3,2},{4,5},{5,4},{6,7},{7,6},{8,9},{9,8},{10,11... | collective-permute-start | bytes 5898248 | tf_op jit(solution)/shard_map/ppermute | solution.py:293
  504.3 80.2 %collective-permute-start.13 = (f32[1920,256]{1,0:T(8,128)}, f32[1920,256]{1,0:T(8,128)}, u32[]{:S(2)}, u32[]{:S(2)}) collective-permute-start(f32[1920,256]{1,0:T(8,128)} %get-tuple-element.70.own_ref), channel_id=1, source_target_pairs={{0,1},{1,0},{2,3},{3,2},{4,5},{5,4},{6,7},{7,6},{8,9},{9,8},{10,11... | collective-permute-start | bytes 5898248 | tf_op jit(solution)/shard_map/ppermute | solution.py:293
  504.7 81.1 %collective-permute-start.14 = (f32[1920,256]{1,0:T(8,128)}, f32[1920,256]{1,0:T(8,128)}, u32[]{:S(2)}, u32[]{:S(2)}) collective-permute-start(f32[1920,256]{1,0:T(8,128)} %collective-permute-done.12.near_ref), channel_id=1, source_target_pairs={{0,1},{1,0},{2,3},{3,2},{4,5},{5,4},{6,7},{7,6},{8,9},{9,8},{10,11... | collective-permute-start | bytes 5898248 | tf_op jit(solution)/shard_map/ppermute | solution.py:293
  514.4 80.0 %collective-permute-start.51 = (f32[224,1920]{1,0:T(8,128)}, f32[224,1920]{1,0:T(8,128)}, u32[]{:S(2)}, u32[]{:S(2)}) collective-permute-start(f32[224,1920]{1,0:T(8,128)} %get-tuple-element.102), channel_id=1, source_target_pairs={{0,2},{1,3},{2,0},{3,1},{4,6},{5,7},{6,4},{7,5},{8,10},{9,11},{10,... | collective-permute-start | bytes 5160968 | tf_op jit(solution)/shard_map/ppermute | solution.py:293
  535.0 63.9 %collective-permute-start.57 = (f32[224,1920]{1,0:T(8,128)}, f32[224,1920]{1,0:T(8,128)S(1)}, u32[]{:S(2)}, u32[]{:S(2)}) collective-permute-start(f32[224,1920]{1,0:T(8,128)} %get-tuple-element.106), channel_id=1, source_target_pairs={{0,4},{1,5},{2,6},{3,7},{4,0},{5,1},{6,2},{7,3},{8,12},{9,13},{10,... | collective-permute-start | bytes 5160968 | tf_op jit(solution)/shard_map/ppermute | solution.py:293
  560.2 40.8 %collective-permute-start.62 = (f32[224,1920]{1,0:T(8,128)}, f32[224,1920]{1,0:T(8,128)}, u32[]{:S(2)}, u32[]{:S(2)}) collective-permute-start(f32[224,1920]{1,0:T(8,128)} %get-tuple-element.110), channel_id=1, source_target_pairs={{0,2},{1,3},{2,0},{3,1},{4,6},{5,7},{6,4},{7,5},{8,10},{9,11},{10,... | collective-permute-start | bytes 5160968 | tf_op jit(solution)/shard_map/ppermute | solution.py:293
  584.5 40.8 %collective-permute-start.67 = (f32[224,1920]{1,0:T(8,128)}, f32[224,1920]{1,0:T(8,128)}, u32[]{:S(2)}, u32[]{:S(2)}) collective-permute-start(f32[224,1920]{1,0:T(8,128)} %get-tuple-element.114), channel_id=1, source_target_pairs={{0,4},{1,5},{2,6},{3,7},{4,0},{5,1},{6,2},{7,3},{8,12},{9,13},{10,... | collective-permute-start | bytes 5160968 | tf_op jit(solution)/shard_map/ppermute | solution.py:293
  585.8 76.4 %collective-permute-start.45 = (f32[224,1920]{1,0:T(8,128)}, f32[224,1920]{1,0:T(8,128)}, u32[]{:S(2)}, u32[]{:S(2)}) collective-permute-start(f32[224,1920]{1,0:T(8,128)} %get-tuple-element.98), channel_id=1, source_target_pairs={{0,4},{1,5},{2,6},{3,7},{4,0},{5,1},{6,2},{7,3},{8,12},{9,13},{10,... | collective-permute-start | bytes 5160968 | tf_op jit(solution)/shard_map/ppermute | solution.py:293
  594.4 71.9 %collective-permute-start.40 = (f32[224,1920]{1,0:T(8,128)}, f32[224,1920]{1,0:T(8,128)S(1)}, u32[]{:S(2)}, u32[]{:S(2)}) collective-permute-start(f32[224,1920]{1,0:T(8,128)} %get-tuple-element.93), channel_id=1, source_target_pairs={{0,2},{1,3},{2,0},{3,1},{4,6},{5,7},{6,4},{7,5},{8,10},{9,11},{10,... | collective-permute-start | bytes 5160968 | tf_op jit(solution)/shard_map/ppermute | solution.py:293
  598.9 100.0 %collective-permute-start.35 = (f32[224,1920]{1,0:T(8,128)S(1)}, f32[224,1920]{1,0:T(8,128)S(1)}, u32[]{:S(2)}, u32[]{:S(2)}) collective-permute-start(f32[224,1920]{1,0:T(8,128)S(1)} %copy-done.37), channel_id=1, source_target_pairs={{0,4},{1,5},{2,6},{3,7},{4,0},{5,1},{6,2},{7,3},{8,12},{9,13},{10,... | collective-permute-start | bytes 5160968 | tf_op jit(solution)/shard_map/ppermute | solution.py:293
  601.4 100.2 %collective-permute-start.30 = (f32[224,1920]{1,0:T(8,128)S(1)}, f32[224,1920]{1,0:T(8,128)S(1)}, u32[]{:S(2)}, u32[]{:S(2)}) collective-permute-start(f32[224,1920]{1,0:T(8,128)S(1)} %copy-done.35), channel_id=1, source_target_pairs={{0,2},{1,3},{2,0},{3,1},{4,6},{5,7},{6,4},{7,5},{8,10},{9,11},{10,... | collective-permute-start | bytes 5160968 | tf_op jit(solution)/shard_map/ppermute | solution.py:293
  625.3 110.5 %collective-permute-start.25 = (f32[224,1920]{1,0:T(8,128)S(1)}, f32[224,1920]{1,0:T(8,128)S(1)}, u32[]{:S(2)}, u32[]{:S(2)}) collective-permute-start(f32[224,1920]{1,0:T(8,128)S(1)} %copy-done.34), channel_id=1, source_target_pairs={{0,4},{1,5},{2,6},{3,7},{4,0},{5,1},{6,2},{7,3},{8,12},{9,13},{10,... | collective-permute-start | bytes 5160968 | tf_op jit(solution)/shard_map/ppermute | solution.py:293
  662.2 75.1 %collective-permute-start.18 = (f32[224,1920]{1,0:T(8,128)S(1)}, f32[224,1920]{1,0:T(8,128)S(1)}, u32[]{:S(2)}, u32[]{:S(2)}) collective-permute-start(f32[224,1920]{1,0:T(8,128)S(1)} %copy-done.36), channel_id=1, source_target_pairs={{0,2},{1,3},{2,0},{3,1},{4,6},{5,7},{6,4},{7,5},{8,10},{9,11},{10,... | collective-permute-start | bytes 5160968 | tf_op jit(solution)/shard_map/ppermute | solution.py:293
  666.3 40.2 %collective-permute-start.11 = (f32[256,896]{0,1:T(8,128)S(1)}, f32[256,896]{0,1:T(8,128)S(1)}, u32[]{:S(2)}, u32[]{:S(2)}) collective-permute-start(f32[256,896]{0,1:T(8,128)S(1)} %add.195), channel_id=1, source_target_pairs={{0,16},{8,24},{16,0},{24,8},{1,17},{9,25},{17,1},{25,9},{2,18},{10... | collective-permute-start | bytes 2752520 | tf_op jit(solution)/shard_map/ppermute | solution.py:293
  698.9 55.4 %collective-permute-start.52 = (f32[112,1920]{1,0:T(8,128)S(1)}, f32[112,1920]{1,0:T(8,128)}, u32[]{:S(2)}, u32[]{:S(2)}) collective-permute-start(f32[112,1920]{1,0:T(8,128)S(1)} %get-tuple-element.136), channel_id=1, source_target_pairs={{0,4},{1,5},{2,6},{3,7},{4,0},{5,1},{6,2},{7,3},{8,12},{9,13},{10,... | collective-permute-start | bytes 2580488 | tf_op jit(solution)/shard_map/ppermute | solution.py:293
  701.6 53.9 %collective-permute-start.58 = (f32[112,1920]{1,0:T(8,128)S(1)}, f32[112,1920]{1,0:T(8,128)}, u32[]{:S(2)}, u32[]{:S(2)}) collective-permute-start(f32[112,1920]{1,0:T(8,128)S(1)} %get-tuple-element.134), channel_id=1, source_target_pairs={{0,2},{1,3},{2,0},{3,1},{4,6},{5,7},{6,4},{7,5},{8,10},{9,11},{10,... | collective-permute-start | bytes 2580488 | tf_op jit(solution)/shard_map/ppermute | solution.py:293
  706.5 66.3 %collective-permute-start.63 = (f32[112,1920]{1,0:T(8,128)S(1)}, f32[112,1920]{1,0:T(8,128)}, u32[]{:S(2)}, u32[]{:S(2)}) collective-permute-start(f32[112,1920]{1,0:T(8,128)S(1)} %get-tuple-element.132), channel_id=1, source_target_pairs={{0,4},{1,5},{2,6},{3,7},{4,0},{5,1},{6,2},{7,3},{8,12},{9,13},{10,... | collective-permute-start | bytes 2580488 | tf_op jit(solution)/shard_map/ppermute | solution.py:293
  735.8 38.2 %collective-permute-start.68 = (f32[112,1920]{1,0:T(8,128)S(1)}, f32[112,1920]{1,0:T(8,128)}, u32[]{:S(2)}, u32[]{:S(2)}) collective-permute-start(f32[112,1920]{1,0:T(8,128)S(1)} %get-tuple-element.130), channel_id=1, source_target_pairs={{0,2},{1,3},{2,0},{3,1},{4,6},{5,7},{6,4},{7,5},{8,10},{9,11},{10,... | collective-permute-start | bytes 2580488 | tf_op jit(solution)/shard_map/ppermute | solution.py:293
  737.3 39.0 %collective-permute-start.46 = (f32[112,1920]{1,0:T(8,128)S(1)}, f32[112,1920]{1,0:T(8,128)}, u32[]{:S(2)}, u32[]{:S(2)}) collective-permute-start(f32[112,1920]{1,0:T(8,128)S(1)} %get-tuple-element.138), channel_id=1, source_target_pairs={{0,2},{1,3},{2,0},{3,1},{4,6},{5,7},{6,4},{7,5},{8,10},{9,11},{10,... | collective-permute-start | bytes 2580488 | tf_op jit(solution)/shard_map/ppermute | solution.py:293
  754.3 79.5 %collective-permute-start.41 = (f32[112,1920]{1,0:T(8,128)}, f32[112,1920]{1,0:T(8,128)}, u32[]{:S(2)}, u32[]{:S(2)}) collective-permute-start(f32[112,1920]{1,0:T(8,128)} %get-tuple-element.140), channel_id=1, source_target_pairs={{0,4},{1,5},{2,6},{3,7},{4,0},{5,1},{6,2},{7,3},{8,12},{9,13},{10,... | collective-permute-start | bytes 2580488 | tf_op jit(solution)/shard_map/ppermute | solution.py:293
  755.6 80.9 %collective-permute-start.36 = (f32[112,1920]{1,0:T(8,128)}, f32[112,1920]{1,0:T(8,128)}, u32[]{:S(2)}, u32[]{:S(2)}) collective-permute-start(f32[112,1920]{1,0:T(8,128)} %get-tuple-element.142), channel_id=1, source_target_pairs={{0,2},{1,3},{2,0},{3,1},{4,6},{5,7},{6,4},{7,5},{8,10},{9,11},{10,... | collective-permute-start | bytes 2580488 | tf_op jit(solution)/shard_map/ppermute | solution.py:293
  772.7 66.4 %collective-permute-start.31 = (f32[112,1920]{1,0:T(8,128)}, f32[112,1920]{1,0:T(8,128)}, u32[]{:S(2)}, u32[]{:S(2)}) collective-permute-start(f32[112,1920]{1,0:T(8,128)} %get-tuple-element.144), channel_id=1, source_target_pairs={{0,4},{1,5},{2,6},{3,7},{4,0},{5,1},{6,2},{7,3},{8,12},{9,13},{10,... | collective-permute-start | bytes 2580488 | tf_op jit(solution)/shard_map/ppermute | solution.py:293
  774.0 67.8 %collective-permute-start.26 = (f32[112,1920]{1,0:T(8,128)}, f32[112,1920]{1,0:T(8,128)}, u32[]{:S(2)}, u32[]{:S(2)}) collective-permute-start(f32[112,1920]{1,0:T(8,128)} %get-tuple-element.146), channel_id=1, source_target_pairs={{0,2},{1,3},{2,0},{3,1},{4,6},{5,7},{6,4},{7,5},{8,10},{9,11},{10,... | collective-permute-start | bytes 2580488 | tf_op jit(solution)/shard_map/ppermute | solution.py:293
  776.3 68.2 %collective-permute-start.19 = (f32[112,1920]{1,0:T(8,128)}, f32[112,1920]{1,0:T(8,128)}, u32[]{:S(2)}, u32[]{:S(2)}) collective-permute-start(f32[112,1920]{1,0:T(8,128)} %get-tuple-element.148), channel_id=1, source_target_pairs={{0,4},{1,5},{2,6},{3,7},{4,0},{5,1},{6,2},{7,3},{8,12},{9,13},{10,... | collective-permute-start | bytes 2580488 | tf_op jit(solution)/shard_map/ppermute | solution.py:293
  (43 other events, 983.4 us)
